TPU v7x, 256 devices: a whole 4x4x8 slice. The times are simulated.
256 devices in a mesh: freq: 32 (over x, z), pts: 8 (over y, core).
Axes of the slice: x: 4, y: 4, z: 8, core: 2. Of those that a mesh axis runs over, the one named last changes fastest.
Arguments:
- snapshots: float32 [256, 5, 65536], P(None, None, ('pts', 'freq')), may hold values from -6 to 6
- weights: float32 [65536], P(('pts', 'freq')), may hold values from 0.25 to 4
- starts: int32 [3], replicated, may hold values from 0 to 128
- bins: int32 [64], replicated, may hold values from 0 to 63, each once
Outputs:
- modes: float32 [64, 2, 5, 65536], P('freq', None, None, 'pts')
- energy: float32 [64], P('freq')
All inputs are finite; a program needn't handle non-finite values.
Results may differ from a plain program's by a relative error of at most 0.00024.
Values sent between devices are 32-bit elements; how exact they have to be, the bound alone decides.
No kernel may reach another device: no remote copies, remote signals or barrier semaphores. Data moves between devices by JAX's collectives and lax.ppermute only.
A program may use at most 64 MiB of HBM per device.

v0:
```python
import math

import jax
import jax.numpy as jnp
from jax import lax
from jax.sharding import Mesh
from jax.sharding import PartitionSpec as P

NFFT = 128
ITERS = 8
FREQ = ("freq_0", "freq_1")
PTS = ("pts_0", "pts_1")
PTS_FREQ = ("pts_0", "pts_1", "freq_0", "freq_1")


def from_everyone(value, axis):
    length = lax.axis_size(axis)
    return lax.all_to_all(
        jnp.broadcast_to(value[None], (length, *value.shape)), axis, 0, 0, tiled=True
    )


def taken_together(value, axis):
    return from_everyone(value, axis).sum(axis=0)


def by_axis(value, axes):
    far, near = axes
    return taken_together(taken_together(value, near), far)


def in_one(arrays, axis):
    ends = [0]
    for a in arrays:
        ends.append(ends[-1] + a.size)
    total = by_axis(jnp.concatenate([a.ravel() for a in arrays]), axis)
    return tuple((total[b:e].reshape(a.shape) for a, b, e in zip(arrays, ends, ends[1:])))


def dft_tables(bins, nfft):
    steps_i = jnp.arange(nfft, dtype=jnp.int32)
    steps_t = steps_i.astype(jnp.float32)
    window = 0.5 - 0.5 * jnp.cos(2.0 * math.pi * steps_t / nfft)
    scale = 1.0 / jnp.sqrt(jnp.sum(window * window))
    phase = (bins[:, None] * steps_i[None, :] % nfft).astype(jnp.float32) * (2.0 * math.pi / nfft)
    return jnp.stack([jnp.cos(phase) * window * scale, -jnp.sin(phase) * window * scale])


def gram_of(spec, wts, count):
    weighted = spec * wts
    real_part = jnp.einsum("kacvp,kbcvp->kab", weighted, spec, precision=lax.Precision.HIGHEST)
    cross = jnp.einsum(
        "kavp,kbvp->kab", weighted[:, :, 0], spec[:, :, 1], precision=lax.Precision.HIGHEST
    )
    return (real_part / count, (cross - jnp.swapaxes(cross, 1, 2)) / count)


def apply_gram(gram_re, gram_im, xr, xi):
    ur = jnp.sum(gram_re * xr[:, None, :], 2) - jnp.sum(gram_im * xi[:, None, :], 2)
    ui = jnp.sum(gram_re * xi[:, None, :], 2) + jnp.sum(gram_im * xr[:, None, :], 2)
    return (ur, ui)


def leading(gram_re, gram_im):
    xr = jnp.ones(gram_re.shape[:2], gram_re.dtype)
    xi = jnp.zeros(gram_re.shape[:2], gram_re.dtype)
    for step in range(ITERS):
        ur, ui = apply_gram(gram_re, gram_im, xr, xi)
        scale_now = jnp.sqrt(jnp.sum(ur * ur + ui * ui, 1))[:, None]
        xr, xi = (ur / scale_now, ui / scale_now)
    ur, ui = apply_gram(gram_re, gram_im, xr, xi)
    return (xr, xi, jnp.sum(xr * ur + xi * ui, 1))


def build_modes(spec, xr, xi, energy):
    hp = lax.Precision.HIGHEST
    real_part = jnp.einsum("kb,kbvp->kvp", xr, spec[:, :, 0], precision=hp) - jnp.einsum(
        "kb,kbvp->kvp", xi, spec[:, :, 1], precision=hp
    )
    imag_part = jnp.einsum("kb,kbvp->kvp", xr, spec[:, :, 1], precision=hp) + jnp.einsum(
        "kb,kbvp->kvp", xi, spec[:, :, 0], precision=hp
    )
    factor = 1.0 / jnp.sqrt(jnp.maximum(energy, 0.25))
    return jnp.stack([real_part, imag_part], 1) * factor[:, None, None, None]


def body(snapshots, weights, starts, bins):
    n_time, n_var, n_local = snapshots.shape
    n_blocks = starts.shape[0]
    centered = snapshots - jnp.mean(snapshots, 0, keepdims=True)
    flat = centered.reshape(n_time, n_var * n_local)
    segments = jnp.stack(
        [lax.dynamic_slice_in_dim(flat, starts[block], NFFT, 0) for block in range(n_blocks)]
    )
    tables = dft_tables(bins, NFFT)
    spec = jnp.einsum("ckt,btn->kbcn", tables, segments, precision=lax.Precision.HIGHEST)
    spec = spec.reshape(bins.shape[0], n_blocks, 2, n_var, n_local)
    total_points = n_local * lax.axis_size(FREQ) * lax.axis_size(PTS)
    count = float(total_points * n_var)
    gram_re, gram_im = gram_of(spec, weights, count)
    gram_re, gram_im = in_one((gram_re, gram_im), (("freq_0", "freq_1"), ("pts_0", "pts_1")))
    xr, xi, energy_all = leading(gram_re, gram_im)
    local_modes = build_modes(spec, xr, xi, energy_all)
    modes = lax.all_to_all(local_modes, FREQ, split_axis=0, concat_axis=3, tiled=True)
    per_dev = bins.shape[0] // lax.axis_size(FREQ)
    energy = lax.dynamic_slice_in_dim(energy_all, lax.axis_index(FREQ) * per_dev, per_dev, 0)
    return (modes, energy)


def solution(mesh):
    split = Mesh(mesh.devices.reshape(4, 8, 4, 2), ("freq_0", "freq_1", "pts_0", "pts_1"))
    placed = (P(None, None, PTS_FREQ), P(PTS_FREQ), P(), P())
    return jax.shard_map(
        body,
        mesh=split,
        in_specs=placed,
        out_specs=(P(FREQ, None, None, PTS), P(FREQ)),
        check_vma=False,
    )
```

profile of v0, /device:TPU:32, one launch (start us, length us, event | category | flops | bytes accessed | tf_op | source)
XLA Modules:
  0.0 114.8 jit_solution(1240332461384616292)
XLA Ops:
  0.6 1.5 %fusion.27 = (s32[1]{0:T(128)}, s32[1]{0:T(128)}, s32[1]{0:T(128)}) fusion(s32[3]{0:T(128)} %param.6), kind=kLoop, calls=%fused_computation.112 | loop fusion | bytes 24 | tf_op jit(solution)/shard_map/slice | solution.py:93
  6.1 0.7 multiply_reduce_fusion.34
  6.8 1.7 %copy.61 = f32[256,5,256]{0,2,1:T(8,128)S(1)} copy(f32[256,5,256]{2,0,1:T(8,128)} %param.4) | data formatting | bytes 2621440 | tf_op args[0]
  11.4 1.1 copy.62
  12.8 1.1 copy.64
  14.7 2.9 %convolution_bitcast_fusion = f32[64,3,2,1280]{3,0,2,1:T(8,128)S(1)} fusion(f32[1,128,1280]{2,1,0:T(8,128)} %bitcast.82, f32[1,128,1280]{2,1,0:T(8,128)S(1)} %bitcast.81, f32[1,128,1280]{2,1,0:T(8,128)S(1)} %bitcast.80, f32[1,64,128]{2,1,0:T(8,128)S(1)} %get-tuple-element.86, f32[1,64,128]{2,1,0:T(8,128)S(1)} %get-tuple-element.85), kind=kOutput, calls=%fused_computation | convolution fusion | flops 755974144 | bytes 3997696 | tf_op jit(solution)/shard_map/ckt,btn->kbcn/dot_general | solution.py:96
  17.7 2.0 %reshape.510 = f32[64,3,2,5,256]{4,3,0,2,1:T(8,128)} reshape(f32[64,3,2,1280]{3,0,2,1:T(8,128)S(1)} %convolution_bitcast_fusion) | data formatting | bytes 3932160 | tf_op jit(solution)/shard_map/reshape | solution.py:97
  19.6 3.6 %broadcast_multiply_fusion = (f32[64,3,2,5,256]{4,1,3,0,2:T(4,128)S(1)}, f32[64,3,2,5,256]{4,1,3,0,2:T(4,128)S(1)}) fusion(f32[256]{0:T(256)S(1)} %copy-done.3, f32[64,3,2,5,256]{4,3,0,2,1:T(8,128)} %reshape.510), kind=kLoop, calls=%fused_computation.10 | loop fusion | flops 491520 | bytes 5899264 | tf_op jit(solution)/shard_map/mul | solution.py:50
  23.2 10.7 %fusion.6 = f32[64,3,3]{2,1,0:T(4,128)S(1)} fusion(f32[64,3,2,5,256]{4,1,3,0,2:T(4,128)S(1)} %get-tuple-element.79, f32[256]{0:T(256)S(1)} %copy-done.3), kind=kOutput, calls=%fused_computation.13 | convolution fusion | flops 18186816 | bytes 1969408 | tf_op jit(solution)/shard_map/kacvp,kbcvp->kab/dot_general | solution.py:51
  34.0 5.5 %fusion.5 = f32[64,3,3]{2,1,0:T(4,128)S(1)} fusion(f32[64,3,2,5,256]{4,1,3,0,2:T(4,128)S(1)} %get-tuple-element.78, f32[64,3,2,5,256]{4,1,3,0,2:T(4,128)S(1)} %get-tuple-element.79), kind=kOutput, calls=%fused_computation.11 | convolution fusion | flops 8847360 | bytes 2623744 | tf_op jit(solution)/shard_map/kavp,kbvp->kab/dot_general | solution.py:52
  40.6 9.7 %all_to_all.30 = f32[8,1,1152]{2,1,0:T(1,128)S(1)} all-to-all(f32[8,1,1152]{2,1,0:T(1,128)S(1)} %broadcast_in_dim.4), channel_id=1, replica_groups=mesh['freq_0'=4,'freq_1'=8,'pts_0'=4,'pts_1'=2] {'pts_0','pts_1'}, dimensions={0} | all-to-all | bytes 73728 | tf_op jit(solution)/shard_map/all_to_all | solution.py:18
  50.3 0.7 broadcast_in_dim.5
  51.1 11.2 %all-to-all-start.1 = ((f32[32,1,1152]{2,1,0:T(1,128)}), f32[32,1,1152]{2,1,0:T(1,128)S(1)}, u32[]{:S(2)}, u32[]{:S(2)}) async-start(f32[32,1,1152]{2,1,0:T(1,128)} %broadcast_in_dim.5), calls=%async_computation.1 | async-start | bytes 294912 | tf_op jit(solution)/shard_map/all_to_all | solution.py:18
  62.3 2.7 %slice_bitcast_fusion = f32[64,3,5,256]{3,2,0,1:T(8,128)} fusion(f32[64,3,2,5,256]{4,3,0,2,1:T(8,128)} %reshape.510), kind=kLoop, calls=%fused_computation.6 | loop fusion | bytes 1966080 | tf_op jit(solution)/shard_map/squeeze | solution.py:77
  64.9 7.3 %all-to-all-done.1 = f32[32,1,1152]{2,1,0:T(1,128)S(1)} async-done(((f32[32,1,1152]{2,1,0:T(1,128)}), f32[32,1,1152]{2,1,0:T(1,128)S(1)}, u32[]{:S(2)}, u32[]{:S(2)}) %all-to-all-start.1) | async-done | bytes 147488 | tf_op jit(solution)/shard_map/all_to_all | solution.py:18
  78.0 2.3 %fusion.11 = f32[64,1,5,256]{3,1,2,0:T(1,128)S(1)} fusion(f32[64,3,1,1]{1,2,3,0:T(1,128)S(1)} %bitcast.83, f32[64,3,2,5,256]{4,1,3,0,2:T(4,128)S(1)} %get-tuple-element.79), kind=kOutput, calls=%fused_computation.18 | convolution fusion | flops 2949120 | bytes 1671168 | tf_op jit(solution)/shard_map/kb,kbvp->kvp/dot_general | solution.py:80
  80.3 2.7 %fusion.9 = f32[64,1,5,256]{3,1,2,0:T(1,128)S(1)} fusion(f32[64,3,1,1]{1,2,3,0:T(1,128)S(1)} %bitcast.84, f32[64,3,5,256]{3,2,0,1:T(8,128)S(1)} %copy-done), kind=kOutput, calls=%fused_computation.16 | convolution fusion | flops 2949120 | bytes 1311488 | tf_op jit(solution)/shard_map/kb,kbvp->kvp/dot_general | solution.py:77
  83.0 2.3 %fusion.12 = f32[64,1,5,256]{3,1,2,0:T(1,128)S(1)} fusion(f32[64,3,1,1]{1,2,3,0:T(1,128)S(1)} %bitcast.85, f32[64,3,2,5,256]{4,1,3,0,2:T(4,128)S(1)} %get-tuple-element.79), kind=kOutput, calls=%fused_computation.19 | convolution fusion | flops 2949120 | bytes 1671168 | tf_op jit(solution)/shard_map/kb,kbvp->kvp/dot_general | solution.py:77
  85.2 3.0 %fusion.7 = f32[64,1,5,256]{3,1,2,0:T(1,128)S(1)} fusion(f32[64,3,1,1]{1,2,3,0:T(1,128)S(1)} %bitcast.86, f32[64,3,5,256]{3,2,0,1:T(8,128)S(1)} %copy-done), kind=kOutput, calls=%fused_computation.14 | convolution fusion | flops 2949120 | bytes 1311488 | tf_op jit(solution)/shard_map/kb,kbvp->kvp/dot_general | solution.py:80
  88.6 1.3 %copy.71 = f32[64,2,5,256]{3,1,2,0:T(2,128)} copy(f32[64,2,5,256]{3,0,2,1:T(8,128)S(1)} %maximum_multiply_fusion) | data formatting | bytes 1310720 | tf_op jit(solution)/shard_map/mul | solution.py:84
  89.9 4.3 %all-to-all-start.2 = ((f32[64,2,5,256]{3,1,2,0:T(2,128)}), f32[64,2,5,256]{3,1,2,0:T(2,128)S(1)}, u32[]{:S(2)}, u32[]{:S(2)}) async-start(f32[64,2,5,256]{3,1,2,0:T(2,128)} %copy.71), calls=%async_computation.2 | async-start | bytes 1310720 | tf_op jit(solution)/shard_map/all_to_all | solution.py:104
  94.3 0.6 dynamic_slice.15
  94.9 18.8 %all-to-all-done.2 = f32[64,2,5,256]{3,1,2,0:T(2,128)S(1)} async-done(((f32[64,2,5,256]{3,1,2,0:T(2,128)}), f32[64,2,5,256]{3,1,2,0:T(2,128)S(1)}, u32[]{:S(2)}, u32[]{:S(2)}) %all-to-all-start.2) | async-done | bytes 655392 | tf_op jit(solution)/shard_map/all_to_all | solution.py:104
  113.6 1.1 copy.87
  (66 shorter events, 8.4 us)
Async XLA Ops:
  0.6 7.9 %copy-start.1 = (f32[256,5,256]{2,0,1:T(8,128)S(1)}, f32[256,5,256]{2,0,1:T(8,128)}, u32[]{:S(2)}) copy-start(f32[256,5,256]{2,0,1:T(8,128)} %param.4) | copy-start | bytes 3932164
  11.4 3.1 %copy-start.4 = (s32[64]{0:T(128)S(1)}, s32[64]{0:T(128)}, u32[]{:S(2)}) copy-start(s32[64]{0:T(128)} %param.7) | copy-start | bytes 772
  12.5 2.2 %copy-start.2 = (f32[128,1280]{1,0:T(8,128)S(1)}, f32[128,1280]{1,0:T(8,128)}, u32[]{:S(2)}) copy-start(f32[128,1280]{1,0:T(8,128)} %copy.62) | copy-start | bytes 1966084
  17.7 2.0 %copy-start.3 = (f32[256]{0:T(256)S(1)}, f32[256]{0:T(256)}, u32[]{:S(2)}) copy-start(f32[256]{0:T(256)} %param.5) | copy-start | bytes 3076
  51.1 21.2 %all-to-all-start.1 = ((f32[32,1,1152]{2,1,0:T(1,128)}), f32[32,1,1152]{2,1,0:T(1,128)S(1)}, u32[]{:S(2)}, u32[]{:S(2)}) async-start(f32[32,1,1152]{2,1,0:T(1,128)} %broadcast_in_dim.5), calls=%async_computation.1 | async-start | bytes 294912 | tf_op jit(solution)/shard_map/all_to_all | solution.py:18
  76.3 3.9 %copy-start = (f32[64,3,5,256]{3,2,0,1:T(8,128)S(1)}, f32[64,3,5,256]{3,2,0,1:T(8,128)}, u32[]{:S(2)}) copy-start(f32[64,3,5,256]{3,2,0,1:T(8,128)} %slice_bitcast_fusion) | copy-start | bytes 2949124
  89.9 23.7 %all-to-all-start.2 = ((f32[64,2,5,256]{3,1,2,0:T(2,128)}), f32[64,2,5,256]{3,1,2,0:T(2,128)S(1)}, u32[]{:S(2)}, u32[]{:S(2)}) async-start(f32[64,2,5,256]{3,1,2,0:T(2,128)} %copy.71), calls=%async_computation.2 | async-start | bytes 1310720 | tf_op jit(solution)/shard_map/all_to_all | solution.py:104
where the time goes:
time: 115 us
  matrix products  29.4 us (26%)
  waiting for transfers between devices  26.1 us (23%)
  local copies, waits for them, and re-layouts  16.1 us (14%)
  starting transfers between devices  15.5 us (13%)
  other arithmetic  10.2 us (9%)
  blocking collectives  9.74 us (8%)
  between operations  7.66 us (7%)
    all_to_all x1, waiting for transfers between devices, body(): lax.all_to_all(local_modes, FREQ, split_axis=0, concat_axis=3, tiled=True)  18.8 us
    all_to_all x1, starting transfers between devices, from_everyone(): lax.all_to_all(jnp.broadcast_to(value[None], (length, *value.shape)), axi...  11.2 us
    dot_general x1, matrix products, gram_of(): jnp.einsum('kacvp,kbcvp->kab', weighted, spec, precision=lax.Precision.HI...  10.7 us
    all_to_all x1, blocking collectives, from_everyone(): lax.all_to_all(jnp.broadcast_to(value[None], (length, *value.shape)), axi...  9.74 us
    all_to_all x1, waiting for transfers between devices, from_everyone(): lax.all_to_all(jnp.broadcast_to(value[None], (length, *value.shape)), axi...  7.35 us
    dot_general x1, matrix products, gram_of(): jnp.einsum('kavp,kbvp->kab', weighted[:, :, 0], spec[:, :, 1], precision=...  5.51 us
    all_to_all x1, starting transfers between devices, body(): lax.all_to_all(local_modes, FREQ, split_axis=0, concat_axis=3, tiled=True)  4.33 us
    mul x1, other arithmetic, gram_of(): weighted = spec * wts  3.58 us
  transfers between devices with their start and end apart: 2, of which 2 were waited for; matrix products, arithmetic and copies ran while one was open for 3% of the time, Pallas kernels for 0%

commit v1 on v0

v1 whole, which is shorter than its diff:
```python
import math

import jax
import jax.numpy as jnp
from jax import lax
from jax.experimental import pallas as pl
from jax.experimental.pallas import tpu as pltpu
from jax.sharding import Mesh
from jax.sharding import PartitionSpec as P

NFFT = 128
NB = 3
ITERS = 8
KF = 64
LANES = 128
QS = 9
PAIRS = ((0, 1), (0, 2), (1, 2))
FREQ = ("freq_0", "freq_1")
PTS = ("pts_0", "pts_1")
PTS_FREQ = ("pts_0", "pts_1", "freq_0", "freq_1")
FIRST = ("freq_0", "pts_0")
SECOND = ("freq_1", "pts_1")


def halves(value):
    high = value.astype(jnp.bfloat16)
    return high, (value - high.astype(jnp.float32)).astype(jnp.bfloat16)


def product(a_high, a_low, b_high, b_low):
    def dot(a, b):
        return jnp.dot(a, b, preferred_element_type=jnp.float32)

    return dot(a_high, b_high) + dot(a_high, b_low) + dot(a_low, b_high)


def column(row, n):
    rows = lax.broadcasted_iota(jnp.int32, (n, n), 0)
    cols = lax.broadcasted_iota(jnp.int32, (n, n), 1)
    wide = jnp.broadcast_to(row, (n, n))
    return jnp.sum(jnp.where(rows == cols, wide, jnp.zeros_like(wide)), axis=1, keepdims=True)


def tables(starts_ref, bins, tab_ref):
    step = lax.broadcasted_iota(jnp.int32, (KF, NFFT), 1)
    angle = 2.0 * math.pi / NFFT
    scale = 1.0 / math.sqrt(sum((0.5 - 0.5 * math.cos(angle * t)) ** 2 for t in range(NFFT)))
    window = (0.5 - 0.5 * jnp.cos(step.astype(jnp.float32) * angle)) * scale
    slot_bins = column(bins.astype(jnp.float32), KF).astype(jnp.int32)
    phase = ((slot_bins * step) & (NFFT - 1)).astype(jnp.float32) * angle
    parts = (jnp.cos(phase) * window, -jnp.sin(phase) * window)
    zero = jnp.zeros((KF, NFFT), jnp.float32)
    for b in range(NB):
        start = starts_ref[b]
        for c in range(2):
            turned = pltpu.roll(parts[c], start & (NFFT - 1), 1)
            tab_ref[2 * b + c, :, :NFFT] = jnp.where(step >= start, turned, zero)
            tab_ref[2 * b + c, :, NFFT:] = jnp.where(step < start, turned, zero)


def spectra_kernel(
    starts_ref, bins_ref, wts_ref, x_hbm, gram_ref, high_ref, low_ref, tab_ref, x_ref, spec_ref,
    prod_ref, sems,
):
    n_var, n_time, n_pts = x_ref.shape
    copies = [pltpu.make_async_copy(x_hbm.at[v], x_ref.at[v], sems.at[v]) for v in range(n_var)]
    for copy in copies:
        copy.start()
    tables(starts_ref, bins_ref[...], tab_ref)
    t_high, t_low = halves(tab_ref[...].reshape(2 * NB * KF, n_time))
    for v in range(n_var):
        copies[v].wait()
        x = x_ref[v]
        high, low = halves(x - jnp.sum(x, axis=0, keepdims=True) * (1.0 / n_time))
        high_ref[v] = high
        low_ref[v] = low
        spec_ref[v] = product(t_high, t_low, high, low)

    def rows(tile, carry):
        first = pl.multiple_of(tile * 8, 8)
        totals = [None] * QS
        for lane in range(0, n_pts, LANES):
            sums = [None] * QS

            def put(q, value):
                sums[q] = value if sums[q] is None else sums[q] + value

            for v in range(n_var):
                s = [
                    spec_ref[v, pl.ds(KF * r + first, 8), lane : lane + LANES]
                    for r in range(2 * NB)
                ]
                re, im = s[0::2], s[1::2]
                for a in range(NB):
                    put(a, re[a] * re[a] + im[a] * im[a])
                for q, (a, c) in enumerate(PAIRS):
                    put(NB + q, re[a] * re[c] + im[a] * im[c])
                    put(2 * NB + q, re[a] * im[c] - im[a] * re[c])
            w = wts_ref[:, lane : lane + LANES]
            for q in range(QS):
                part = sums[q] * w
                totals[q] = part if totals[q] is None else totals[q] + part
        for q in range(QS):
            prod_ref[pl.ds(KF * q + first, 8), :] = totals[q]
        return carry

    lax.fori_loop(0, KF // 8, rows, 0)
    sums = lax.dot_general(
        jnp.ones((8, LANES), jnp.float32),
        prod_ref[...],
        (((1,), (1,)), ((), ())),
        precision=lax.Precision.HIGHEST,
        preferred_element_type=jnp.float32,
    )
    gram_ref[...] = jnp.broadcast_to(sums[0:1][None], gram_ref.shape)


def relay_kernel(in_ref, out_ref):
    out_ref[...] = jnp.broadcast_to(jnp.sum(in_ref[...], axis=0, keepdims=True), out_ref.shape)


def leading(grams):
    diag, cross_re, cross_im = grams[:NB], grams[NB : 2 * NB], grams[2 * NB :]
    place = {p: q for q, p in enumerate(PAIRS)}

    def apply(xr, xi):
        ur, ui = [], []
        for a in range(NB):
            r, i = diag[a] * xr[a], diag[a] * xi[a]
            for c in range(NB):
                if c == a:
                    continue
                g = cross_re[place[min(a, c), max(a, c)]]
                h = cross_im[place[min(a, c), max(a, c)]]
                if a < c:
                    r, i = r + (g * xr[c] - h * xi[c]), i + (g * xi[c] + h * xr[c])
                else:
                    r, i = r + (g * xr[c] + h * xi[c]), i + (g * xi[c] - h * xr[c])
            ur.append(r)
            ui.append(i)
        return ur, ui

    xr = [jnp.ones_like(diag[0])] * NB
    xi = [jnp.zeros_like(diag[0])] * NB
    for _ in range(ITERS):
        ur, ui = apply(xr, xi)
        size = sum(r * r + i * i for r, i in zip(ur, ui))
        inverse = lax.rsqrt(size)
        xr, xi = [r * inverse for r in ur], [i * inverse for i in ui]
    ur, ui = apply(xr, xi)
    return xr, xi, sum(a * b + c * d for a, b, c, d in zip(xr, ur, xi, ui))


def modes_kernel(count, in_ref, tab_ref, high_ref, low_ref, modes_ref, energy_ref):
    n_var, n_time, n_pts = high_ref.shape
    total = jnp.sum(in_ref[...], axis=0) * (1.0 / count)
    xr, xi, energy = leading([total[:, KF * q : KF * (q + 1)] for q in range(QS)])
    energy_ref[...] = energy
    factor = lax.rsqrt(jnp.maximum(energy, 0.25))
    cr = [column(x * factor, KF) for x in xr]
    ci = [column(x * factor, KF) for x in xi]
    m_re = m_im = None
    for b in range(NB):
        t_re, t_im = tab_ref[2 * b], tab_ref[2 * b + 1]
        re = cr[b] * t_re - ci[b] * t_im
        im = cr[b] * t_im + ci[b] * t_re
        m_re = re if m_re is None else m_re + re
        m_im = im if m_im is None else m_im + im
    m_high, m_low = halves(jnp.concatenate([m_re, m_im], axis=0))
    tiles = n_pts // LANES
    stride = 2 * n_var * tiles
    for v in range(n_var):
        out = product(m_high, m_low, high_ref[v], low_ref[v])
        for t in range(tiles):
            for c in range(2):
                modes_ref[pl.ds(2 * (v * tiles + t) + c, KF, stride), :] = out[
                    KF * c : KF * (c + 1), LANES * t : LANES * (t + 1)
                ]


def spectra(starts, bins, weights, x, peers):
    n_var, n_time, n_pts = x.shape
    vmem, smem = pltpu.VMEM, pltpu.SMEM
    spec = pl.BlockSpec
    return pl.pallas_call(
        spectra_kernel,
        in_specs=[
            spec(memory_space=smem), spec(memory_space=vmem), spec(memory_space=vmem),
            spec(memory_space=pl.ANY),
        ],
        out_specs=[spec(memory_space=vmem)] * 4,
        out_shape=[
            jax.ShapeDtypeStruct((peers, 1, QS * KF), jnp.float32),
            jax.ShapeDtypeStruct(x.shape, jnp.bfloat16),
            jax.ShapeDtypeStruct(x.shape, jnp.bfloat16),
            jax.ShapeDtypeStruct((2 * NB, KF, n_time), jnp.float32),
        ],
        scratch_shapes=[
            vmem(x.shape, jnp.float32),
            vmem((n_var, 2 * NB * KF, n_pts), jnp.float32),
            vmem((QS * KF, LANES), jnp.float32),
            pltpu.SemaphoreType.DMA((n_var,)),
        ],
        name="spectra",
    )(starts, bins, weights, x)


def body(snapshots, weights, starts, bins):
    n_time, n_var, n_pts = snapshots.shape
    tiles = n_pts // LANES
    n_freq = lax.axis_size(FREQ)
    per_dev = bins.shape[0] // n_freq
    count = float(n_pts * n_freq * lax.axis_size(PTS) * n_var)
    first, second = lax.axis_size(FIRST), lax.axis_size(SECOND)
    gram, high, low, tab = spectra(
        starts, bins[None], weights[None], jnp.transpose(snapshots, (1, 0, 2)), first
    )
    gram = lax.all_to_all(gram, FIRST, 0, 0, tiled=True)
    gram = pl.pallas_call(
        relay_kernel,
        out_shape=jax.ShapeDtypeStruct((second, 1, QS * KF), jnp.float32),
        name="relay",
    )(gram)
    gram = lax.all_to_all(gram, SECOND, 0, 0, tiled=True)
    rows = 2 * n_var * tiles
    vmem = pltpu.VMEM
    modes, energy_all = pl.pallas_call(
        lambda *refs: modes_kernel(count, *refs),
        in_specs=[pl.BlockSpec(memory_space=vmem)] * 4,
        out_specs=[pl.BlockSpec(memory_space=vmem)] * 2,
        out_shape=[
            jax.ShapeDtypeStruct((KF * rows, LANES), jnp.float32),
            jax.ShapeDtypeStruct((1, KF), jnp.float32),
        ],
        name="modes",
    )(gram, tab, high, low)
    modes = modes.reshape(n_freq, per_dev * rows, LANES)
    modes = lax.all_to_all(modes, FREQ, 0, 0, tiled=True)
    modes = modes.reshape(n_freq, per_dev, n_var, tiles, 2, LANES)
    modes = jnp.transpose(modes, (1, 4, 2, 0, 3, 5))
    modes = modes.reshape(per_dev, 2, n_var, n_freq * n_pts)
    energy = lax.dynamic_slice_in_dim(energy_all[0], lax.axis_index(FREQ) * per_dev, per_dev, 0)
    return (modes, energy)


def solution(mesh):
    split = Mesh(mesh.devices.reshape(4, 8, 4, 2), ("freq_0", "freq_1", "pts_0", "pts_1"))
    placed = (P(None, None, PTS_FREQ), P(PTS_FREQ), P(), P())
    return jax.shard_map(
        body,
        mesh=split,
        in_specs=placed,
        out_specs=(P(FREQ, None, None, PTS), P(FREQ)),
        check_vma=False,
    )
```

time: 115 us -> 71.6 us (0.62)
  matrix products: 29.4 us -> 0 us
  blocking collectives: 9.74 us -> 29.8 us
  local copies, waits for them, and re-layouts: 16.1 us -> 2.51 us
  Pallas kernels: 0 us -> 12.7 us
  starting transfers between devices: 15.5 us -> 5.19 us
  other arithmetic: 10.2 us -> 0 us
  between operations: 7.66 us -> 0.67 us
  waiting for transfers between devices: 26.1 us -> 20.3 us
    dot_general x7 -> x0, matrix products: 29.4 us -> none  [the longest x1 10.7 us: gram_of(): jnp.einsum('kacvp,kbcvp->kab', weighted, spec, precision=lax.Precision.HI...]
    all_to_all x1 -> x2, blocking collectives: 9.74 us -> 29.8 us  [the longest x1 15 us: body(): gram = lax.all_to_all(gram, SECOND, 0, 0, tiled=True)]
    pallas_call x0 -> x3, Pallas kernels: none -> 12.7 us  [the longest x1 5.91 us: spectra(): pl.pallas_call(spectra_kernel, in_specs=[spec(memory_space=smem), spec(me...]
    all_to_all x2 -> x1, starting transfers between devices: 15.5 us -> 5.19 us  [body(): modes = lax.all_to_all(modes, FREQ, 0, 0, tiled=True)]
    all_to_all x2 -> x1, waiting for transfers between devices: 26.1 us -> 20.3 us  [body(): modes = lax.all_to_all(modes, FREQ, 0, 0, tiled=True)]
    reduce_sum x22 -> x0, other arithmetic: 5.05 us -> none  [the longest x8 2.81 us: apply_gram(): jnp.sum(gram_re * xr[:, None, :], 2) - jnp.sum(gram_im * xi[:, None, :], 2)]
    mul x3 -> x0, other arithmetic: 3.91 us -> none  [the longest x1 3.58 us: gram_of(): weighted = spec * wts]
    dynamic_slice x5 -> x1, local copies, waits for them, and re-layouts: 3.54 us -> 0.59 us  [body(): lax.dynamic_slice_in_dim(energy_all[0], lax.axis_index(FREQ) * per_dev, p...]
  transfers between devices with their start and end apart: 2 -> 1, of which waited for: 2 -> 1; matrix products, arithmetic and copies ran while one was open for 3% -> 1% of each run, Pallas kernels for 0% -> 0%
where the time goes in v1:
time: 71.6 us; the launch traced here: 71.2 us
  blocking collectives  29.8 us (42%)
  waiting for transfers between devices  20.3 us (28%)
  Pallas kernels  12.7 us (18%)
  starting transfers between devices  5.19 us (7%)
  local copies, waits for them, and re-layouts  2.51 us (4%)
    all_to_all x1, waiting for transfers between devices, body(): modes = lax.all_to_all(modes, FREQ, 0, 0, tiled=True)  20.3 us
    all_to_all x1, blocking collectives, body(): gram = lax.all_to_all(gram, SECOND, 0, 0, tiled=True)  15 us
    all_to_all x1, blocking collectives, body(): gram = lax.all_to_all(gram, FIRST, 0, 0, tiled=True)  14.8 us
    pallas_call x1, Pallas kernels, spectra(): pl.pallas_call(spectra_kernel, in_specs=[spec(memory_space=smem), spec(me...  5.91 us
    pallas_call x1, Pallas kernels, body(): pl.pallas_call(lambda *refs: modes_kernel(count, *refs), in_specs=[pl.Blo...  5.35 us
    all_to_all x1, starting transfers between devices, body(): modes = lax.all_to_all(modes, FREQ, 0, 0, tiled=True)  5.19 us
    reshape x1, local copies, waits for them, and re-layouts, body(): modes = modes.reshape(per_dev, 2, n_var, n_freq * n_pts)  1.59 us
  transfers between devices with their start and end apart: 1, of which 1 were waited for; matrix products, arithmetic and copies ran while one was open for 1% of the time, Pallas kernels for 0%

profile of v1, /device:TPU:32, one launch (start us, length us, event | category | flops | bytes accessed | tf_op | source)
XLA Modules:
  0.0 71.2 jit_solution(158970643939170570)
XLA Ops:
  0.6 5.9 %spectra.1 = (f32[16,1,576]{2,1,0:T(1,128)}, bf16[5,256,256]{2,1,0:T(8,128)(2,1)}, bf16[5,256,256]{2,1,0:T(8,128)(2,1)}, f32[6,64,256]{2,1,0:T(8,128)}) custom-call(s32[3]{0:T(128)} %starts_ref.1, s32[1,64]{1,0:T(1,128)} %bitcast.17, f32[1,256]{1,0:T(1,128)} %bitcast.16, f32[5,256,256]{2,1,0:T(8,128)} %bitcast.14), custom_call_target="tpu_custom_call" | custom-call | tf_op jit(solution)/shard_map/spectra/pallas_call | solution.py:185
  6.6 14.8 %all_to_all.15.in_ref = f32[16,1,576]{2,1,0:T(1,128)} all-to-all(f32[16,1,576]{2,1,0:T(1,128)} %get-tuple-element.8), channel_id=1, replica_groups=mesh['freq_0'=4,'freq_1'=8,'pts_0'=4,'pts_1'=2] {'freq_0','pts_0'}, dimensions={0} | all-to-all | bytes 73728 | tf_op jit(solution)/shard_map/all_to_all | solution.py:218
  21.3 1.4 %relay.1 = f32[16,1,576]{2,1,0:T(1,128)} custom-call(f32[16,1,576]{2,1,0:T(1,128)} %all_to_all.15.in_ref), custom_call_target="tpu_custom_call" | custom-call | tf_op jit(solution)/shard_map/relay/pallas_call | solution.py:219
  22.8 15.0 %all_to_all.16.refs_0_ = f32[16,1,576]{2,1,0:T(1,128)} all-to-all(f32[16,1,576]{2,1,0:T(1,128)} %relay.1), channel_id=1, replica_groups=mesh['freq_0'=4,'freq_1'=8,'pts_0'=4,'pts_1'=2] {'freq_1','pts_1'}, dimensions={0} | all-to-all | bytes 73728 | tf_op jit(solution)/shard_map/all_to_all | solution.py:224
  37.8 5.4 %modes.1 = (f32[1280,128]{1,0:T(8,128)}, f32[1,64]{1,0:T(1,128)}) custom-call(f32[16,1,576]{2,1,0:T(1,128)} %all_to_all.16.refs_0_, f32[6,64,256]{2,1,0:T(8,128)} %get-tuple-element.9.refs_1_, bf16[5,256,256]{2,1,0:T(8,128)(2,1)} %get-tuple-element.10.refs_2_, bf16[5,256,256]{2,1,0:T(8,128)(2,1)} %get-tuple-element.11.refs_3_), custom_call_target="tpu_custom_call" | custom-call | tf_op jit(solution)/shard_map/modes/pallas_call | solution.py:227
  43.1 0.0 copy-start
  43.1 5.2 %all-to-all-start.2 = ((f32[32,40,128]{2,1,0:T(8,128)}), f32[32,40,128]{2,1,0:T(8,128)S(1)}, u32[]{:S(2)}, u32[]{:S(2)}) async-start(f32[32,40,128]{2,1,0:T(8,128)} %bitcast.15), calls=%async_computation.2 | async-start | bytes 1310720 | tf_op jit(solution)/shard_map/all_to_all | solution.py:238
  48.3 0.0 copy-done
  48.3 0.6 dynamic-slice_bitcast_fusion
  48.9 20.3 %all-to-all-done.2 = f32[32,40,128]{2,1,0:T(8,128)S(1)} async-done(((f32[32,40,128]{2,1,0:T(8,128)}), f32[32,40,128]{2,1,0:T(8,128)S(1)}, u32[]{:S(2)}, u32[]{:S(2)}) %all-to-all-start.2) | async-done | bytes 655392 | tf_op jit(solution)/shard_map/all_to_all | solution.py:238
  69.3 0.3 copy.8
  69.6 1.6 %reshape.16 = f32[2,2,5,8192]{3,1,2,0:T(2,128)} reshape(f32[2,2,5,32,2,128]{5,4,3,1,2,0:T(2,128)S(1)} %bitcast.13) | data formatting | bytes 1310720 | tf_op jit(solution)/shard_map/reshape | solution.py:241
Async XLA Ops:
  43.1 5.2 %copy-start = (f32[1,64]{1,0:T(1,128)S(1)}, f32[1,64]{1,0:T(1,128)}, u32[]{:S(2)}) copy-start(f32[1,64]{1,0:T(1,128)} %get-tuple-element.13) | copy-start | bytes 772
  43.1 26.1 %all-to-all-start.2 = ((f32[32,40,128]{2,1,0:T(8,128)}), f32[32,40,128]{2,1,0:T(8,128)S(1)}, u32[]{:S(2)}, u32[]{:S(2)}) async-start(f32[32,40,128]{2,1,0:T(8,128)} %bitcast.15), calls=%async_computation.2 | async-start | bytes 1310720 | tf_op jit(solution)/shard_map/all_to_all | solution.py:238

commit v2 on v1

--- a/solution.py
+++ b/solution.py
@@ -1,3 +1,4 @@
+import functools
 import math
 
 import jax
@@ -41,14 +42,38 @@
     return jnp.sum(jnp.where(rows == cols, wide, jnp.zeros_like(wide)), axis=1, keepdims=True)
 
 
+def series(square, terms):
+    total = jnp.full_like(square, terms[-1])
+    for term in terms[-2::-1]:
+        total = total * square + term
+    return total
+
+
+def circle(turns):
+    quarter = NFFT // 4
+    shifted = turns + quarter // 2
+    small = (shifted & (quarter - 1)) - quarter // 2
+    side = (shifted >> int(math.log2(quarter))) & 3
+    angle = small.astype(jnp.float32) * (2.0 * math.pi / NFFT)
+    square = angle * angle
+    cos = series(square, [(-1.0) ** n / math.factorial(2 * n) for n in range(6)])
+    sin = angle * series(square, [(-1.0) ** n / math.factorial(2 * n + 1) for n in range(6)])
+    swap = (side & 1) == 1
+    first, second = jnp.where(swap, sin, cos), jnp.where(swap, cos, sin)
+    return (
+        jnp.where((side == 1) | (side == 2), -first, first),
+        jnp.where(side >= 2, -second, second),
+    )
+
+
 def tables(starts_ref, bins, tab_ref):
     step = lax.broadcasted_iota(jnp.int32, (KF, NFFT), 1)
     angle = 2.0 * math.pi / NFFT
     scale = 1.0 / math.sqrt(sum((0.5 - 0.5 * math.cos(angle * t)) ** 2 for t in range(NFFT)))
-    window = (0.5 - 0.5 * jnp.cos(step.astype(jnp.float32) * angle)) * scale
+    window = ((0.5 - 0.5 * circle(step[:8])[0]) * scale)[:1]
     slot_bins = column(bins.astype(jnp.float32), KF).astype(jnp.int32)
-    phase = ((slot_bins * step) & (NFFT - 1)).astype(jnp.float32) * angle
-    parts = (jnp.cos(phase) * window, -jnp.sin(phase) * window)
+    cos, sin = circle(slot_bins * step)
+    parts = (cos * window, -sin * window)
     zero = jnp.zeros((KF, NFFT), jnp.float32)
     for b in range(NB):
         start = starts_ref[b]
@@ -59,17 +84,22 @@
 
 
 def spectra_kernel(
-    starts_ref, bins_ref, wts_ref, x_hbm, gram_ref, high_ref, low_ref, tab_ref, x_ref, spec_ref,
-    prod_ref, sems,
+    starts_hbm, bins_hbm, wts_hbm, x_hbm, gram_ref, high_ref, low_ref, tab_ref, x_ref, starts_ref,
+    bins_ref, wts_ref, spec_ref, prod_ref, sems,
 ):
     n_var, n_time, n_pts = x_ref.shape
-    copies = [pltpu.make_async_copy(x_hbm.at[v], x_ref.at[v], sems.at[v]) for v in range(n_var)]
+    moves = [(starts_hbm, starts_ref), (bins_hbm, bins_ref)]
+    moves += [(x_hbm.at[v], x_ref.at[v]) for v in range(n_var)] + [(wts_hbm, wts_ref)]
+    copies = [pltpu.make_async_copy(a, b, sems.at[i]) for i, (a, b) in enumerate(moves)]
     for copy in copies:
         copy.start()
+    copies[0].wait()
+    copies[1].wait()
     tables(starts_ref, bins_ref[...], tab_ref)
     t_high, t_low = halves(tab_ref[...].reshape(2 * NB * KF, n_time))
+    for copy in copies[2:]:
+        copy.wait()
     for v in range(n_var):
-        copies[v].wait()
         x = x_ref[v]
         high, low = halves(x - jnp.sum(x, axis=0, keepdims=True) * (1.0 / n_time))
         high_ref[v] = high
@@ -105,12 +135,10 @@
         return carry
 
     lax.fori_loop(0, KF // 8, rows, 0)
-    sums = lax.dot_general(
-        jnp.ones((8, LANES), jnp.float32),
-        prod_ref[...],
-        (((1,), (1,)), ((), ())),
-        precision=lax.Precision.HIGHEST,
-        preferred_element_type=jnp.float32,
+    ones = jnp.ones((16, LANES), jnp.bfloat16)
+    sums = sum(
+        lax.dot_general(ones, p, (((1,), (1,)), ((), ())), preferred_element_type=jnp.float32)
+        for p in halves(prod_ref[...])
     )
     gram_ref[...] = jnp.broadcast_to(sums[0:1][None], gram_ref.shape)
 
@@ -154,11 +182,24 @@
 def modes_kernel(count, in_ref, tab_ref, high_ref, low_ref, modes_ref, energy_ref):
     n_var, n_time, n_pts = high_ref.shape
     total = jnp.sum(in_ref[...], axis=0) * (1.0 / count)
-    xr, xi, energy = leading([total[:, KF * q : KF * (q + 1)] for q in range(QS)])
-    energy_ref[...] = energy
+    wide = []
+    for first in range(0, QS * KF, LANES):
+        part = total[:, first : first + LANES]
+        if part.shape[1] == LANES:
+            wide += [part, pltpu.roll(part, KF, 1)]
+        else:
+            wide.append(jnp.concatenate([part, part], axis=1))
+    xr, xi, energy = leading(wide)
+    per_dev = energy_ref.shape[1]
+    shift = lax.rem(LANES - lax.axis_index(FREQ) * per_dev, LANES)
+    energy_ref[...] = pltpu.roll(energy, shift, 1)[:, :per_dev]
     factor = lax.rsqrt(jnp.maximum(energy, 0.25))
-    cr = [column(x * factor, KF) for x in xr]
-    ci = [column(x * factor, KF) for x in xi]
+    zero = jnp.zeros_like(factor)
+    turned = jnp.transpose(
+        jnp.concatenate([x * factor for x in xr + xi] + [zero, zero], axis=0)
+    )
+    cr = [turned[:KF, b : b + 1] for b in range(NB)]
+    ci = [turned[:KF, NB + b : NB + b + 1] for b in range(NB)]
     m_re = m_im = None
     for b in range(NB):
         t_re, t_im = tab_ref[2 * b], tab_ref[2 * b + 1]
@@ -178,28 +219,39 @@
                 ]
 
 
+def assemble_kernel(in_ref, out_hbm, sems):
+    copies = [
+        pltpu.make_async_copy(in_ref.at[:, g], out_hbm.at[g], sems.at[g])
+        for g in range(out_hbm.shape[0])
+    ]
+    for copy in copies:
+        copy.start()
+    for copy in copies:
+        copy.wait()
+
+
 def spectra(starts, bins, weights, x, peers):
     n_var, n_time, n_pts = x.shape
     vmem, smem = pltpu.VMEM, pltpu.SMEM
     spec = pl.BlockSpec
     return pl.pallas_call(
         spectra_kernel,
-        in_specs=[
-            spec(memory_space=smem), spec(memory_space=vmem), spec(memory_space=vmem),
-            spec(memory_space=pl.ANY),
-        ],
+        in_specs=[spec(memory_space=pl.ANY)] * 4,
         out_specs=[spec(memory_space=vmem)] * 4,
         out_shape=[
-            jax.ShapeDtypeStruct((peers, 1, QS * KF), jnp.float32),
-            jax.ShapeDtypeStruct(x.shape, jnp.bfloat16),
-            jax.ShapeDtypeStruct(x.shape, jnp.bfloat16),
-            jax.ShapeDtypeStruct((2 * NB, KF, n_time), jnp.float32),
+            vmem((peers, 1, QS * KF), jnp.float32),
+            vmem(x.shape, jnp.bfloat16),
+            vmem(x.shape, jnp.bfloat16),
+            vmem((2 * NB, KF, n_time), jnp.float32),
         ],
         scratch_shapes=[
             vmem(x.shape, jnp.float32),
+            smem(starts.shape, jnp.int32),
+            vmem(bins.shape, jnp.int32),
+            vmem(weights.shape, jnp.float32),
             vmem((n_var, 2 * NB * KF, n_pts), jnp.float32),
             vmem((QS * KF, LANES), jnp.float32),
-            pltpu.SemaphoreType.DMA((n_var,)),
+            pltpu.SemaphoreType.DMA((n_var + 3,)),
         ],
         name="spectra",
     )(starts, bins, weights, x)
@@ -215,32 +267,40 @@
     gram, high, low, tab = spectra(
         starts, bins[None], weights[None], jnp.transpose(snapshots, (1, 0, 2)), first
     )
+    vmem = pltpu.VMEM
+    keep = functools.partial(pltpu.with_memory_space_constraint, memory_space=vmem)
+    in_vmem = pl.BlockSpec(memory_space=vmem)
     gram = lax.all_to_all(gram, FIRST, 0, 0, tiled=True)
     gram = pl.pallas_call(
         relay_kernel,
-        out_shape=jax.ShapeDtypeStruct((second, 1, QS * KF), jnp.float32),
+        in_specs=[in_vmem],
+        out_specs=in_vmem,
+        out_shape=vmem((second, 1, QS * KF), jnp.float32),
         name="relay",
-    )(gram)
+    )(keep(gram))
     gram = lax.all_to_all(gram, SECOND, 0, 0, tiled=True)
     rows = 2 * n_var * tiles
-    vmem = pltpu.VMEM
-    modes, energy_all = pl.pallas_call(
-        lambda *refs: modes_kernel(count, *refs),
-        in_specs=[pl.BlockSpec(memory_space=vmem)] * 4,
-        out_specs=[pl.BlockSpec(memory_space=vmem)] * 2,
-        out_shape=[
-            jax.ShapeDtypeStruct((KF * rows, LANES), jnp.float32),
-            jax.ShapeDtypeStruct((1, KF), jnp.float32),
-        ],
+    modes, energy = pl.pallas_call(
+        functools.partial(modes_kernel, count),
+        in_specs=[in_vmem] * 4,
+        out_specs=[in_vmem] * 2,
+        out_shape=[vmem((KF * rows, LANES), jnp.float32), jax.ShapeDtypeStruct((1, per_dev), jnp.float32)],
         name="modes",
-    )(gram, tab, high, low)
-    modes = modes.reshape(n_freq, per_dev * rows, LANES)
+    )(keep(gram), keep(tab), keep(high), keep(low))
+    groups = per_dev * n_var
+    modes = modes.reshape(n_freq, groups, 2 * tiles, LANES)
     modes = lax.all_to_all(modes, FREQ, 0, 0, tiled=True)
-    modes = modes.reshape(n_freq, per_dev, n_var, tiles, 2, LANES)
-    modes = jnp.transpose(modes, (1, 4, 2, 0, 3, 5))
-    modes = modes.reshape(per_dev, 2, n_var, n_freq * n_pts)
-    energy = lax.dynamic_slice_in_dim(energy_all[0], lax.axis_index(FREQ) * per_dev, per_dev, 0)
-    return (modes, energy)
+    modes = pl.pallas_call(
+        assemble_kernel,
+        in_specs=[in_vmem],
+        out_specs=pl.BlockSpec(memory_space=pl.ANY),
+        out_shape=jax.ShapeDtypeStruct((groups, n_freq, 2 * tiles, LANES), jnp.float32),
+        scratch_shapes=[pltpu.SemaphoreType.DMA((groups,))],
+        name="assemble",
+    )(keep(modes))
+    modes = modes.reshape(per_dev, n_var, n_freq * tiles, 2, LANES)
+    modes = jnp.transpose(modes, (0, 3, 1, 2, 4)).reshape(per_dev, 2, n_var, n_freq * n_pts)
+    return (modes, energy[0])
 
 
 def solution(mesh):

time: 71.6 us -> 60.4 us (0.84)
  blocking collectives: 29.8 us -> 54.3 us
  waiting for transfers between devices: 20.3 us -> 0 us
  Pallas kernels: 12.7 us -> 5.19 us
  starting transfers between devices: 5.19 us -> 0 us
  local copies, waits for them, and re-layouts: 2.51 us -> 0 us
    all_to_all x0 -> x1, blocking collectives: none -> 25.2 us  [body(): modes = lax.all_to_all(modes, FREQ, 0, 0, tiled=True)]
    all_to_all x1 -> x0, waiting for transfers between devices: 20.3 us -> none  [body(): modes = lax.all_to_all(modes, FREQ, 0, 0, tiled=True)]
    pallas_call x3 -> x4, Pallas kernels: 12.7 us -> 5.19 us  [the longest x1 3.25 us: spectra(): pl.pallas_call(spectra_kernel, in_specs=[spec(memory_space=pl.ANY)] * 4,...]
    all_to_all x1 -> x0, starting transfers between devices: 5.19 us -> none  [body(): modes = lax.all_to_all(modes, FREQ, 0, 0, tiled=True)]
    reshape x2 -> x0, local copies, waits for them, and re-layouts: 1.92 us -> none  [the longest x1 1.59 us: body(): modes = modes.reshape(per_dev, 2, n_var, n_freq * n_pts)]
  transfers between devices with their start and end apart: 1 -> 0, of which waited for: 1 -> 0; matrix products, arithmetic and copies ran while one was open for 1% -> 0% of each run, Pallas kernels for 0% -> 0%
where the time goes in v2:
time: 60.4 us; the launch traced here: 60.1 us
  blocking collectives  54.3 us (90%)
  Pallas kernels  5.19 us (9%)
  between operations  0.64 us (1%)
    all_to_all x1, blocking collectives, body(): modes = lax.all_to_all(modes, FREQ, 0, 0, tiled=True)  25.2 us
    all_to_all x1, blocking collectives, body(): gram = lax.all_to_all(gram, SECOND, 0, 0, tiled=True)  14.7 us
    all_to_all x1, blocking collectives, body(): gram = lax.all_to_all(gram, FIRST, 0, 0, tiled=True)  14.5 us
    pallas_call x1, Pallas kernels, spectra(): pl.pallas_call(spectra_kernel, in_specs=[spec(memory_space=pl.ANY)] * 4,...  3.25 us

profile of v2, /device:TPU:32, one launch (start us, length us, event | category | flops | bytes accessed | tf_op | source)
XLA Modules:
  0.0 60.1 jit_solution(8975166749490547921)
XLA Ops:
  0.6 3.3 %spectra.1 = (f32[16,1,576]{2,1,0:T(1,128)S(1)}, bf16[5,256,256]{2,1,0:T(8,128)(2,1)S(1)}, bf16[5,256,256]{2,1,0:T(8,128)(2,1)S(1)}, f32[6,64,256]{2,1,0:T(8,128)S(1)}) custom-call(s32[3]{0:T(128)} %starts_hbm.1, s32[1,64]{1,0:T(1,128)} %bitcast.14, f32[1,256]{1,0:T(1,128)} %bitcast.13, f32[5,256,256]{2,1,0:T(8,128)} %bitcast.11), custom_call_target="tpu_custom_call" | custom-call | tf_op jit(solution)/shard_map/spectra/pallas_call | solution.py:237
  3.9 14.5 %all_to_all.15.in_ref = f32[16,1,576]{2,1,0:T(1,128)S(1)} all-to-all(f32[16,1,576]{2,1,0:T(1,128)S(1)} %get-tuple-element.8), channel_id=1, replica_groups=mesh['freq_0'=4,'freq_1'=8,'pts_0'=4,'pts_1'=2] {'freq_0','pts_0'}, dimensions={0} | all-to-all | bytes 73728 | tf_op jit(solution)/shard_map/all_to_all | solution.py:273
  18.4 14.7 %all_to_all.16.in_ref = f32[16,1,576]{2,1,0:T(1,128)S(1)} all-to-all(f32[16,1,576]{2,1,0:T(1,128)S(1)} %relay.1), channel_id=1, replica_groups=mesh['freq_0'=4,'freq_1'=8,'pts_0'=4,'pts_1'=2] {'freq_1','pts_1'}, dimensions={0} | all-to-all | bytes 73728 | tf_op jit(solution)/shard_map/all_to_all | solution.py:281
  33.1 1.0 %modes.1 = (f32[1280,128]{1,0:T(8,128)S(1)}, f32[1,2]{1,0:T(1,128)}) custom-call(f32[16,1,576]{2,1,0:T(1,128)S(1)} %all_to_all.16.in_ref, f32[6,64,256]{2,1,0:T(8,128)S(1)} %get-tuple-element.9.tab_ref, bf16[5,256,256]{2,1,0:T(8,128)(2,1)S(1)} %get-tuple-element.10.high_ref, bf16[5,256,256]{2,1,0:T(8,128)(2,1)S(1)} %get-tuple-element.11.low_ref), custom_call_target="tpu_custom_call" | custom-call | tf_op jit(solution)/shard_map/modes/pallas_call | solution.py:283
  34.1 25.2 %all_to_all.17.in_ref = f32[32,10,4,128]{3,2,1,0:T(4,128)S(1)} all-to-all(f32[32,10,4,128]{3,2,1,0:T(4,128)S(1)} %bitcast.10), channel_id=1, replica_groups=mesh['freq_0'=4,'freq_1'=8,'pts_0'=4,'pts_1'=2] {'freq_0','freq_1'}, dimensions={0} | all-to-all | bytes 1310720 | tf_op jit(solution)/shard_map/all_to_all | solution.py:292
  59.2 0.9 %assemble.1 = f32[10,32,4,128]{3,2,1,0:T(4,128)} custom-call(f32[32,10,4,128]{3,2,1,0:T(4,128)S(1)} %all_to_all.17.in_ref), custom_call_target="tpu_custom_call" | custom-call | tf_op jit(solution)/shard_map/assemble/pallas_call | solution.py:293
  (1 shorter events, 0.0 us)

commit v3 on v2

--- a/solution.py
+++ b/solution.py
@@ -20,7 +20,7 @@
 PTS = ("pts_0", "pts_1")
 PTS_FREQ = ("pts_0", "pts_1", "freq_0", "freq_1")
 FIRST = ("freq_0", "pts_0")
-SECOND = ("freq_1", "pts_1")
+SECOND = ("freq_1",)
 
 
 def halves(value):
@@ -85,7 +85,7 @@
 
 def spectra_kernel(
     starts_hbm, bins_hbm, wts_hbm, x_hbm, gram_ref, high_ref, low_ref, tab_ref, x_ref, starts_ref,
-    bins_ref, wts_ref, spec_ref, prod_ref, sems,
+    bins_ref, wts_ref, spec_ref, sum_ref, sems,
 ):
     n_var, n_time, n_pts = x_ref.shape
     moves = [(starts_hbm, starts_ref), (bins_hbm, bins_ref)]
@@ -105,46 +105,37 @@
         high_ref[v] = high
         low_ref[v] = low
         spec_ref[v] = product(t_high, t_low, high, low)
-
-    def rows(tile, carry):
-        first = pl.multiple_of(tile * 8, 8)
-        totals = [None] * QS
-        for lane in range(0, n_pts, LANES):
-            sums = [None] * QS
-
-            def put(q, value):
-                sums[q] = value if sums[q] is None else sums[q] + value
-
-            for v in range(n_var):
+        for first in range(0, KF, 8):
+            for lane in range(0, n_pts, LANES):
                 s = [
-                    spec_ref[v, pl.ds(KF * r + first, 8), lane : lane + LANES]
+                    spec_ref[v, KF * r + first : KF * r + first + 8, lane : lane + LANES]
                     for r in range(2 * NB)
                 ]
                 re, im = s[0::2], s[1::2]
-                for a in range(NB):
-                    put(a, re[a] * re[a] + im[a] * im[a])
-                for q, (a, c) in enumerate(PAIRS):
-                    put(NB + q, re[a] * re[c] + im[a] * im[c])
-                    put(2 * NB + q, re[a] * im[c] - im[a] * re[c])
-            w = wts_ref[:, lane : lane + LANES]
-            for q in range(QS):
-                part = sums[q] * w
-                totals[q] = part if totals[q] is None else totals[q] + part
-        for q in range(QS):
-            prod_ref[pl.ds(KF * q + first, 8), :] = totals[q]
-        return carry
-
-    lax.fori_loop(0, KF // 8, rows, 0)
+                parts = [re[a] * re[a] + im[a] * im[a] for a in range(NB)]
+                parts += [re[a] * re[c] + im[a] * im[c] for a, c in PAIRS]
+                parts += [re[a] * im[c] - im[a] * re[c] for a, c in PAIRS]
+                for q in range(QS):
+                    if v > 0:
+                        parts[q] = parts[q] + sum_ref[q, first : first + 8, lane : lane + LANES]
+                    sum_ref[q, first : first + 8, lane : lane + LANES] = parts[q]
+    weighted = sum_ref[...] * wts_ref[...][None]
+    prod = sum(weighted[:, :, lane : lane + LANES] for lane in range(0, n_pts, LANES))
+    prod = prod.reshape(QS * KF, LANES)
     ones = jnp.ones((16, LANES), jnp.bfloat16)
     sums = sum(
         lax.dot_general(ones, p, (((1,), (1,)), ((), ())), preferred_element_type=jnp.float32)
-        for p in halves(prod_ref[...])
+        for p in halves(prod)
     )
     gram_ref[...] = jnp.broadcast_to(sums[0:1][None], gram_ref.shape)
 
 
 def relay_kernel(in_ref, out_ref):
     out_ref[...] = jnp.broadcast_to(jnp.sum(in_ref[...], axis=0, keepdims=True), out_ref.shape)
+
+
+def pair_kernel(one_ref, two_ref, out_ref):
+    out_ref[...] = jnp.broadcast_to(one_ref[...] + two_ref[...], out_ref.shape)
 
 
 def leading(grams):
@@ -250,7 +241,7 @@
             vmem(bins.shape, jnp.int32),
             vmem(weights.shape, jnp.float32),
             vmem((n_var, 2 * NB * KF, n_pts), jnp.float32),
-            vmem((QS * KF, LANES), jnp.float32),
+            vmem((QS, KF, n_pts), jnp.float32),
             pltpu.SemaphoreType.DMA((n_var + 3,)),
         ],
         name="spectra",
@@ -265,11 +256,19 @@
     count = float(n_pts * n_freq * lax.axis_size(PTS) * n_var)
     first, second = lax.axis_size(FIRST), lax.axis_size(SECOND)
     gram, high, low, tab = spectra(
-        starts, bins[None], weights[None], jnp.transpose(snapshots, (1, 0, 2)), first
+        starts, bins[None], weights[None], jnp.transpose(snapshots, (1, 0, 2)), 1
     )
     vmem = pltpu.VMEM
     keep = functools.partial(pltpu.with_memory_space_constraint, memory_space=vmem)
     in_vmem = pl.BlockSpec(memory_space=vmem)
+    other = lax.ppermute(gram, "pts_1", [(0, 1), (1, 0)])
+    gram = pl.pallas_call(
+        pair_kernel,
+        in_specs=[in_vmem] * 2,
+        out_specs=in_vmem,
+        out_shape=vmem((first, 1, QS * KF), jnp.float32),
+        name="pair",
+    )(keep(gram), keep(other))
     gram = lax.all_to_all(gram, FIRST, 0, 0, tiled=True)
     gram = pl.pallas_call(
         relay_kernel,

time: 60.4 us -> 58.3 us (0.965)
  blocking collectives: 54.3 us -> 51.4 us
  waiting for transfers between devices: 0 us -> 1.15 us
    all_to_all x1, blocking collectives: 25.2 us -> 22.2 us  [body(): modes = lax.all_to_all(modes, FREQ, 0, 0, tiled=True)]
    ppermute x0 -> x1, waiting for transfers between devices: none -> 1.15 us  [body(): other = lax.ppermute(gram, 'pts_1', [(0, 1), (1, 0)])]
  transfers between devices with their start and end apart: 0 -> 1, of which waited for: 0 -> 1; matrix products, arithmetic and copies ran while one was open for 0% -> 0% of each run, Pallas kernels for 0% -> 0%
where the time goes in v3:
time: 58.3 us; the launch traced here: 58.1 us
  blocking collectives  51.4 us (88%)
  Pallas kernels  4.83 us (8%)
  waiting for transfers between devices  1.15 us (2%)
  between operations  0.65 us (1%)
    all_to_all x1, blocking collectives, body(): modes = lax.all_to_all(modes, FREQ, 0, 0, tiled=True)  22.2 us
    all_to_all x1, blocking collectives, body(): gram = lax.all_to_all(gram, SECOND, 0, 0, tiled=True)  14.8 us
    all_to_all x1, blocking collectives, body(): gram = lax.all_to_all(gram, FIRST, 0, 0, tiled=True)  14.5 us
    pallas_call x1, Pallas kernels, spectra(): pl.pallas_call(spectra_kernel, in_specs=[spec(memory_space=pl.ANY)] * 4,...  2.9 us
  transfers between devices with their start and end apart: 1, of which 1 were waited for; matrix products, arithmetic and copies ran while one was open for 0% of the time, Pallas kernels for 0%

profile of v3, /device:TPU:32, one launch (start us, length us, event | category | flops | bytes accessed | tf_op | source)
XLA Modules:
  0.0 58.1 jit_solution(6673638876315347506)
XLA Ops:
  0.6 2.9 %spectra.1 = (f32[1,1,576]{2,1,0:T(1,128)S(1)}, bf16[5,256,256]{2,1,0:T(8,128)(2,1)S(1)}, bf16[5,256,256]{2,1,0:T(8,128)(2,1)S(1)}, f32[6,64,256]{2,1,0:T(8,128)S(1)}) custom-call(s32[3]{0:T(128)} %starts_hbm.1, s32[1,64]{1,0:T(1,128)} %bitcast.14, f32[1,256]{1,0:T(1,128)} %bitcast.13, f32[5,256,256]{2,1,0:T(8,128)} %bitcast.11), custom_call_target="tpu_custom_call" | custom-call | tf_op jit(solution)/shard_map/spectra/pallas_call | solution.py:228
  3.5 0.1 collective-permute-start
  3.6 1.2 %collective-permute-done.two_ref = f32[1,1,576]{2,1,0:T(1,128)S(1)} collective-permute-done((f32[1,1,576]{2,1,0:T(1,128)S(1)}, f32[1,1,576]{2,1,0:T(1,128)S(1)}, u32[]{:S(2)}, u32[]{:S(2)}) %collective-permute-start) | collective-permute-done | bytes 2336 | tf_op jit(solution)/shard_map/ppermute | solution.py:264
  4.8 14.5 %all_to_all.15.in_ref = f32[16,1,576]{2,1,0:T(1,128)S(1)} all-to-all(f32[16,1,576]{2,1,0:T(1,128)S(1)} %pair.1), channel_id=1, replica_groups=mesh['freq_0'=4,'freq_1'=8,'pts_0'=4,'pts_1'=2] {'freq_0','pts_0'}, dimensions={0} | all-to-all | bytes 73728 | tf_op jit(solution)/shard_map/all_to_all | solution.py:272
  19.3 14.8 %all_to_all.16.in_ref = f32[8,1,576]{2,1,0:T(1,128)S(1)} all-to-all(f32[8,1,576]{2,1,0:T(1,128)S(1)} %relay.1), channel_id=1, replica_groups=mesh['freq_0'=4,'freq_1'=8,'pts_0'=4,'pts_1'=2] {'freq_1'}, dimensions={0} | all-to-all | bytes 36864 | tf_op jit(solution)/shard_map/all_to_all | solution.py:280
  34.1 1.0 %modes.1 = (f32[1280,128]{1,0:T(8,128)S(1)}, f32[1,2]{1,0:T(1,128)}) custom-call(f32[8,1,576]{2,1,0:T(1,128)S(1)} %all_to_all.16.in_ref, f32[6,64,256]{2,1,0:T(8,128)S(1)} %get-tuple-element.9.tab_ref, bf16[5,256,256]{2,1,0:T(8,128)(2,1)S(1)} %get-tuple-element.10.high_ref, bf16[5,256,256]{2,1,0:T(8,128)(2,1)S(1)} %get-tuple-element.11.low_ref), custom_call_target="tpu_custom_call" | custom-call | tf_op jit(solution)/shard_map/modes/pallas_call | solution.py:282
  35.0 22.2 %all_to_all.17.in_ref = f32[32,10,4,128]{3,2,1,0:T(4,128)S(1)} all-to-all(f32[32,10,4,128]{3,2,1,0:T(4,128)S(1)} %bitcast.10), channel_id=1, replica_groups=mesh['freq_0'=4,'freq_1'=8,'pts_0'=4,'pts_1'=2] {'freq_0','freq_1'}, dimensions={0} | all-to-all | bytes 1310720 | tf_op jit(solution)/shard_map/all_to_all | solution.py:291
  57.2 0.9 %assemble.1 = f32[10,32,4,128]{3,2,1,0:T(4,128)} custom-call(f32[32,10,4,128]{3,2,1,0:T(4,128)S(1)} %all_to_all.17.in_ref), custom_call_target="tpu_custom_call" | custom-call | tf_op jit(solution)/shard_map/assemble/pallas_call | solution.py:292
  (2 shorter events, 0.0 us)
Async XLA Ops:
  3.5 1.3 %collective-permute-start = (f32[1,1,576]{2,1,0:T(1,128)S(1)}, f32[1,1,576]{2,1,0:T(1,128)S(1)}, u32[]{:S(2)}, u32[]{:S(2)}) collective-permute-start(f32[1,1,576]{2,1,0:T(1,128)S(1)} %get-tuple-element.8.one_ref), channel_id=1, source_target_pairs={{0,1},{1,0},{2,3},{3,2},{4,5},{5,4},{6,7},{7,6},{8,9},{9,8},{10,11... | collective-permute-start | bytes 6920 | tf_op jit(solution)/shard_map/ppermute | solution.py:264

commit v4 on v3

--- a/solution.py
+++ b/solution.py
@@ -19,8 +19,6 @@
 FREQ = ("freq_0", "freq_1")
 PTS = ("pts_0", "pts_1")
 PTS_FREQ = ("pts_0", "pts_1", "freq_0", "freq_1")
-FIRST = ("freq_0", "pts_0")
-SECOND = ("freq_1",)
 
 
 def halves(value):
@@ -130,14 +128,6 @@
     gram_ref[...] = jnp.broadcast_to(sums[0:1][None], gram_ref.shape)
 
 
-def relay_kernel(in_ref, out_ref):
-    out_ref[...] = jnp.broadcast_to(jnp.sum(in_ref[...], axis=0, keepdims=True), out_ref.shape)
-
-
-def pair_kernel(one_ref, two_ref, out_ref):
-    out_ref[...] = jnp.broadcast_to(one_ref[...] + two_ref[...], out_ref.shape)
-
-
 def leading(grams):
     diag, cross_re, cross_im = grams[:NB], grams[NB : 2 * NB], grams[2 * NB :]
     place = {p: q for q, p in enumerate(PAIRS)}
@@ -168,6 +158,22 @@
         xr, xi = [r * inverse for r in ur], [i * inverse for i in ui]
     ur, ui = apply(xr, xi)
     return xr, xi, sum(a * b + c * d for a, b, c, d in zip(xr, ur, xi, ui))
+
+
+def add_kernel(one_ref, two_ref, out_ref):
+    out_ref[...] = jnp.broadcast_to(one_ref[...] + two_ref[...], out_ref.shape)
+
+
+def add(one, two, copies):
+    in_vmem = pl.BlockSpec(memory_space=pltpu.VMEM)
+    keep = functools.partial(pltpu.with_memory_space_constraint, memory_space=pltpu.VMEM)
+    return pl.pallas_call(
+        add_kernel,
+        in_specs=[in_vmem] * 2,
+        out_specs=in_vmem,
+        out_shape=pltpu.VMEM((copies, *one.shape[1:]), jnp.float32),
+        name="add",
+    )(keep(one), keep(two))
 
 
 def modes_kernel(count, in_ref, tab_ref, high_ref, low_ref, modes_ref, energy_ref):
@@ -210,11 +216,12 @@
                 ]
 
 
-def assemble_kernel(in_ref, out_hbm, sems):
+def assemble_kernel(in_ref, energy_ref, out_hbm, energy_hbm, sems):
+    groups = out_hbm.shape[0]
     copies = [
-        pltpu.make_async_copy(in_ref.at[:, g], out_hbm.at[g], sems.at[g])
-        for g in range(out_hbm.shape[0])
+        pltpu.make_async_copy(in_ref.at[:, g], out_hbm.at[g], sems.at[g]) for g in range(groups)
     ]
+    copies.append(pltpu.make_async_copy(energy_ref, energy_hbm, sems.at[groups]))
     for copy in copies:
         copy.start()
     for copy in copies:
@@ -254,49 +261,39 @@
     n_freq = lax.axis_size(FREQ)
     per_dev = bins.shape[0] // n_freq
     count = float(n_pts * n_freq * lax.axis_size(PTS) * n_var)
-    first, second = lax.axis_size(FIRST), lax.axis_size(SECOND)
     gram, high, low, tab = spectra(
         starts, bins[None], weights[None], jnp.transpose(snapshots, (1, 0, 2)), 1
     )
     vmem = pltpu.VMEM
     keep = functools.partial(pltpu.with_memory_space_constraint, memory_space=vmem)
     in_vmem = pl.BlockSpec(memory_space=vmem)
-    other = lax.ppermute(gram, "pts_1", [(0, 1), (1, 0)])
-    gram = pl.pallas_call(
-        pair_kernel,
-        in_specs=[in_vmem] * 2,
-        out_specs=in_vmem,
-        out_shape=vmem((first, 1, QS * KF), jnp.float32),
-        name="pair",
-    )(keep(gram), keep(other))
-    gram = lax.all_to_all(gram, FIRST, 0, 0, tiled=True)
-    gram = pl.pallas_call(
-        relay_kernel,
-        in_specs=[in_vmem],
-        out_specs=in_vmem,
-        out_shape=vmem((second, 1, QS * KF), jnp.float32),
-        name="relay",
-    )(keep(gram))
-    gram = lax.all_to_all(gram, SECOND, 0, 0, tiled=True)
+    pairings = (("pts_1", 1), ("pts_0", 1), ("pts_0", 3))
+    for step, (axis, flip) in enumerate(pairings, 1):
+        other = lax.ppermute(gram, axis, [(i, i ^ flip) for i in range(lax.axis_size(axis))])
+        gram = add(gram, other, n_freq if step == len(pairings) else 1)
+    gram = lax.all_to_all(gram, FREQ, 0, 0, tiled=True)
     rows = 2 * n_var * tiles
     modes, energy = pl.pallas_call(
         functools.partial(modes_kernel, count),
         in_specs=[in_vmem] * 4,
         out_specs=[in_vmem] * 2,
-        out_shape=[vmem((KF * rows, LANES), jnp.float32), jax.ShapeDtypeStruct((1, per_dev), jnp.float32)],
+        out_shape=[vmem((KF * rows, LANES), jnp.float32), vmem((1, per_dev), jnp.float32)],
         name="modes",
     )(keep(gram), keep(tab), keep(high), keep(low))
     groups = per_dev * n_var
     modes = modes.reshape(n_freq, groups, 2 * tiles, LANES)
     modes = lax.all_to_all(modes, FREQ, 0, 0, tiled=True)
-    modes = pl.pallas_call(
+    modes, energy = pl.pallas_call(
         assemble_kernel,
-        in_specs=[in_vmem],
-        out_specs=pl.BlockSpec(memory_space=pl.ANY),
-        out_shape=jax.ShapeDtypeStruct((groups, n_freq, 2 * tiles, LANES), jnp.float32),
-        scratch_shapes=[pltpu.SemaphoreType.DMA((groups,))],
+        in_specs=[in_vmem] * 2,
+        out_specs=[pl.BlockSpec(memory_space=pl.ANY)] * 2,
+        out_shape=[
+            jax.ShapeDtypeStruct((groups, n_freq, 2 * tiles, LANES), jnp.float32),
+            jax.ShapeDtypeStruct((1, per_dev), jnp.float32),
+        ],
+        scratch_shapes=[pltpu.SemaphoreType.DMA((groups + 1,))],
         name="assemble",
-    )(keep(modes))
+    )(keep(modes), keep(energy))
     modes = modes.reshape(per_dev, n_var, n_freq * tiles, 2, LANES)
     modes = jnp.transpose(modes, (0, 3, 1, 2, 4)).reshape(per_dev, 2, n_var, n_freq * n_pts)
     return (modes, energy[0])

time: 58.3 us -> 56.9 us (0.976)
  blocking collectives: 51.4 us -> 41.7 us
  starting transfers between devices: 0.09 us -> 4.67 us
  waiting for transfers between devices: 1.15 us -> 4.96 us
    all_to_all x2 -> x1, blocking collectives: 29.2 us -> 20.3 us  [body(): gram = lax.all_to_all(gram, FREQ, 0, 0, tiled=True)]
    ppermute x1 -> x3, starting transfers between devices: 0.09 us -> 4.67 us  [body(): lax.ppermute(gram, axis, [(i, i ^ flip) for i in range(lax.axis_size(axis...]
    ppermute x1 -> x3, waiting for transfers between devices: 1.15 us -> 4.96 us  [body(): lax.ppermute(gram, axis, [(i, i ^ flip) for i in range(lax.axis_size(axis...]
    all_to_all x1, blocking collectives: 22.2 us -> 21.4 us  [body(): modes = lax.all_to_all(modes, FREQ, 0, 0, tiled=True)]
  transfers between devices with their start and end apart: 1 -> 3, of which waited for: 1 -> 3; matrix products, arithmetic and copies ran while one was open for 0% -> 0% of each run, Pallas kernels for 0% -> 0%
where the time goes in v4:
time: 56.9 us; the launch traced here: 56.7 us
  blocking collectives  41.7 us (73%)
  waiting for transfers between devices  4.96 us (9%)
  Pallas kernels  4.73 us (8%)
  starting transfers between devices  4.67 us (8%)
  between operations  0.66 us (1%)
    all_to_all x1, blocking collectives, body(): modes = lax.all_to_all(modes, FREQ, 0, 0, tiled=True)  21.4 us
    all_to_all x1, blocking collectives, body(): gram = lax.all_to_all(gram, FREQ, 0, 0, tiled=True)  20.3 us
    ppermute x3, waiting for transfers between devices, body(): lax.ppermute(gram, axis, [(i, i ^ flip) for i in range(lax.axis_size(axis...  4.96 us
    ppermute x3, starting transfers between devices, body(): lax.ppermute(gram, axis, [(i, i ^ flip) for i in range(lax.axis_size(axis...  4.67 us
    pallas_call x1, Pallas kernels, spectra(): pl.pallas_call(spectra_kernel, in_specs=[spec(memory_space=pl.ANY)] * 4,...  2.91 us
  transfers between devices with their start and end apart: 3, of which 3 were waited for; matrix products, arithmetic and copies ran while one was open for 0% of the time, Pallas kernels for 0%

profile of v4, /device:TPU:32, one launch (start us, length us, event | category | flops | bytes accessed | tf_op | source)
XLA Modules:
  0.0 56.7 jit_solution(9044678889401824558)
XLA Ops:
  0.6 2.9 %spectra.1 = (f32[1,1,576]{2,1,0:T(1,128)S(1)}, bf16[5,256,256]{2,1,0:T(8,128)(2,1)S(1)}, bf16[5,256,256]{2,1,0:T(8,128)(2,1)S(1)}, f32[6,64,256]{2,1,0:T(8,128)S(1)}) custom-call(s32[3]{0:T(128)} %starts_hbm.1, s32[1,64]{1,0:T(1,128)} %bitcast.13, f32[1,256]{1,0:T(1,128)} %bitcast.12, f32[5,256,256]{2,1,0:T(8,128)} %bitcast.11), custom_call_target="tpu_custom_call" | custom-call | tf_op jit(solution)/shard_map/spectra/pallas_call | solution.py:235
  3.5 0.1 collective-permute-start
  3.6 1.2 %collective-permute-done.two_ref = f32[1,1,576]{2,1,0:T(1,128)S(1)} collective-permute-done((f32[1,1,576]{2,1,0:T(1,128)S(1)}, f32[1,1,576]{2,1,0:T(1,128)S(1)}, u32[]{:S(2)}, u32[]{:S(2)}) %collective-permute-start) | collective-permute-done | bytes 2336 | tf_op jit(solution)/shard_map/ppermute | solution.py:272
  4.8 1.6 %collective-permute-start.1 = (f32[1,1,576]{2,1,0:T(1,128)S(1)}, f32[1,1,576]{2,1,0:T(1,128)S(1)}, u32[]{:S(2)}, u32[]{:S(2)}) collective-permute-start(f32[1,1,576]{2,1,0:T(1,128)S(1)} %add.3.one_ref), channel_id=1, source_target_pairs={{0,2},{2,0},{4,6},{6,4},{1,3},{3,1},{5,7},{7,5},{8,10},{10,8},{12,... | collective-permute-start | bytes 6920 | tf_op jit(solution)/shard_map/ppermute | solution.py:272
  6.4 2.0 %collective-permute-done.1.two_ref = f32[1,1,576]{2,1,0:T(1,128)S(1)} collective-permute-done((f32[1,1,576]{2,1,0:T(1,128)S(1)}, f32[1,1,576]{2,1,0:T(1,128)S(1)}, u32[]{:S(2)}, u32[]{:S(2)}) %collective-permute-start.1) | collective-permute-done | bytes 2336 | tf_op jit(solution)/shard_map/ppermute | solution.py:272
  8.4 3.0 %collective-permute-start.2 = (f32[1,1,576]{2,1,0:T(1,128)S(1)}, f32[1,1,576]{2,1,0:T(1,128)S(1)}, u32[]{:S(2)}, u32[]{:S(2)}) collective-permute-start(f32[1,1,576]{2,1,0:T(1,128)S(1)} %add.4.one_ref), channel_id=1, source_target_pairs={{0,6},{2,4},{4,2},{6,0},{1,7},{3,5},{5,3},{7,1},{8,14},{10,12},{12... | collective-permute-start | bytes 6920 | tf_op jit(solution)/shard_map/ppermute | solution.py:272
  11.4 1.8 %collective-permute-done.2.two_ref = f32[1,1,576]{2,1,0:T(1,128)S(1)} collective-permute-done((f32[1,1,576]{2,1,0:T(1,128)S(1)}, f32[1,1,576]{2,1,0:T(1,128)S(1)}, u32[]{:S(2)}, u32[]{:S(2)}) %collective-permute-start.2) | collective-permute-done | bytes 2336 | tf_op jit(solution)/shard_map/ppermute | solution.py:272
  13.2 20.3 %all_to_all.10.in_ref = f32[32,1,576]{2,1,0:T(1,128)S(1)} all-to-all(f32[32,1,576]{2,1,0:T(1,128)S(1)} %add.5), channel_id=1, replica_groups=mesh['freq_0'=4,'freq_1'=8,'pts_0'=4,'pts_1'=2] {'freq_0','freq_1'}, dimensions={0} | all-to-all | bytes 147456 | tf_op jit(solution)/shard_map/all_to_all | solution.py:274
  33.5 0.9 %modes.1 = (f32[1280,128]{1,0:T(8,128)S(1)}, f32[1,2]{1,0:T(1,128)S(1)}) custom-call(f32[32,1,576]{2,1,0:T(1,128)S(1)} %all_to_all.10.in_ref, f32[6,64,256]{2,1,0:T(8,128)S(1)} %get-tuple-element.11.tab_ref, bf16[5,256,256]{2,1,0:T(8,128)(2,1)S(1)} %get-tuple-element.12.high_ref, bf16[5,256,256]{2,1,0:T(8,128)(2,1)S(1)} %get-tuple-element.13.low_ref), custom_call_target="tpu_custom_call" | custom-call | tf_op jit(solution)/shard_map/modes/pallas_call | solution.py:276
  34.4 21.4 %all_to_all.11.in_ref = f32[32,10,4,128]{3,2,1,0:T(4,128)S(1)} all-to-all(f32[32,10,4,128]{3,2,1,0:T(4,128)S(1)} %bitcast.10), channel_id=1, replica_groups=mesh['freq_0'=4,'freq_1'=8,'pts_0'=4,'pts_1'=2] {'freq_0','freq_1'}, dimensions={0} | all-to-all | bytes 1310720 | tf_op jit(solution)/shard_map/all_to_all | solution.py:285
  55.8 0.9 %assemble.1 = (f32[10,32,4,128]{3,2,1,0:T(4,128)}, f32[1,2]{1,0:T(1,128)}) custom-call(f32[32,10,4,128]{3,2,1,0:T(4,128)S(1)} %all_to_all.11.in_ref, f32[1,2]{1,0:T(1,128)S(1)} %get-tuple-element.15.energy_ref), custom_call_target="tpu_custom_call" | custom-call | tf_op jit(solution)/shard_map/assemble/pallas_call | solution.py:286
  (3 shorter events, 0.0 us)
Async XLA Ops:
  3.5 1.3 %collective-permute-start = (f32[1,1,576]{2,1,0:T(1,128)S(1)}, f32[1,1,576]{2,1,0:T(1,128)S(1)}, u32[]{:S(2)}, u32[]{:S(2)}) collective-permute-start(f32[1,1,576]{2,1,0:T(1,128)S(1)} %get-tuple-element.10.one_ref), channel_id=1, source_target_pairs={{0,1},{1,0},{2,3},{3,2},{4,5},{5,4},{6,7},{7,6},{8,9},{9,8},{10,11... | collective-permute-start | bytes 6920 | tf_op jit(solution)/shard_map/ppermute | solution.py:272
  4.8 3.6 %collective-permute-start.1 = (f32[1,1,576]{2,1,0:T(1,128)S(1)}, f32[1,1,576]{2,1,0:T(1,128)S(1)}, u32[]{:S(2)}, u32[]{:S(2)}) collective-permute-start(f32[1,1,576]{2,1,0:T(1,128)S(1)} %add.3.one_ref), channel_id=1, source_target_pairs={{0,2},{2,0},{4,6},{6,4},{1,3},{3,1},{5,7},{7,5},{8,10},{10,8},{12,... | collective-permute-start | bytes 6920 | tf_op jit(solution)/shard_map/ppermute | solution.py:272
  8.4 4.8 %collective-permute-start.2 = (f32[1,1,576]{2,1,0:T(1,128)S(1)}, f32[1,1,576]{2,1,0:T(1,128)S(1)}, u32[]{:S(2)}, u32[]{:S(2)}) collective-permute-start(f32[1,1,576]{2,1,0:T(1,128)S(1)} %add.4.one_ref), channel_id=1, source_target_pairs={{0,6},{2,4},{4,2},{6,0},{1,7},{3,5},{5,3},{7,1},{8,14},{10,12},{12... | collective-permute-start | bytes 6920 | tf_op jit(solution)/shard_map/ppermute | solution.py:272

commit v5 on v4

--- a/solution.py
+++ b/solution.py
@@ -31,6 +31,20 @@
         return jnp.dot(a, b, preferred_element_type=jnp.float32)
 
     return dot(a_high, b_high) + dot(a_high, b_low) + dot(a_low, b_high)
+
+
+def thirds(value):
+    high, low = halves(value)
+    rest = value - high.astype(jnp.float32) - low.astype(jnp.float32)
+    return high, low, rest.astype(jnp.bfloat16)
+
+
+def fine_product(a, b):
+    def dot(i, j):
+        return jnp.dot(a[i], b[j], preferred_element_type=jnp.float32)
+
+    small = dot(1, 1) + dot(0, 2) + dot(2, 0)
+    return dot(0, 0) + dot(0, 1) + dot(1, 0) + small
 
 
 def column(row, n):
@@ -82,7 +96,7 @@
 
 
 def spectra_kernel(
-    starts_hbm, bins_hbm, wts_hbm, x_hbm, gram_ref, high_ref, low_ref, tab_ref, x_ref, starts_ref,
+    starts_hbm, bins_hbm, wts_hbm, x_hbm, gram_ref, left_ref, right_ref, tab_ref, x_ref, starts_ref,
     bins_ref, wts_ref, spec_ref, sum_ref, sems,
 ):
     n_var, n_time, n_pts = x_ref.shape
@@ -99,9 +113,9 @@
         copy.wait()
     for v in range(n_var):
         x = x_ref[v]
-        high, low = halves(x - jnp.sum(x, axis=0, keepdims=True) * (1.0 / n_time))
-        high_ref[v] = high
-        low_ref[v] = low
+        centered = x - jnp.sum(x, axis=0, keepdims=True) * (1.0 / n_time)
+        left_ref[v], right_ref[v] = centered[:, : n_pts // 2], centered[:, n_pts // 2 :]
+        high, low = halves(centered)
         spec_ref[v] = product(t_high, t_low, high, low)
         for first in range(0, KF, 8):
             for lane in range(0, n_pts, LANES):
@@ -176,8 +190,8 @@
     )(keep(one), keep(two))
 
 
-def modes_kernel(count, in_ref, tab_ref, high_ref, low_ref, modes_ref, energy_ref):
-    n_var, n_time, n_pts = high_ref.shape
+def modes_kernel(count, in_ref, tab_ref, left_ref, right_ref, modes_ref, energy_ref):
+    n_var, n_time, n_pts = left_ref.shape[0], left_ref.shape[1], 2 * left_ref.shape[2]
     total = jnp.sum(in_ref[...], axis=0) * (1.0 / count)
     wide = []
     for first in range(0, QS * KF, LANES):
@@ -204,11 +218,12 @@
         im = cr[b] * t_im + ci[b] * t_re
         m_re = re if m_re is None else m_re + re
         m_im = im if m_im is None else m_im + im
-    m_high, m_low = halves(jnp.concatenate([m_re, m_im], axis=0))
+    m_parts = thirds(jnp.concatenate([m_re, m_im], axis=0))
     tiles = n_pts // LANES
     stride = 2 * n_var * tiles
     for v in range(n_var):
-        out = product(m_high, m_low, high_ref[v], low_ref[v])
+        centered = jnp.concatenate([left_ref[v], right_ref[v]], axis=1)
+        out = fine_product(m_parts, thirds(centered))
         for t in range(tiles):
             for c in range(2):
                 modes_ref[pl.ds(2 * (v * tiles + t) + c, KF, stride), :] = out[
@@ -238,8 +253,8 @@
         out_specs=[spec(memory_space=vmem)] * 4,
         out_shape=[
             vmem((peers, 1, QS * KF), jnp.float32),
-            vmem(x.shape, jnp.bfloat16),
-            vmem(x.shape, jnp.bfloat16),
+            vmem((n_var, n_time, n_pts // 2), jnp.float32),
+            vmem((n_var, n_time, n_pts // 2), jnp.float32),
             vmem((2 * NB, KF, n_time), jnp.float32),
         ],
         scratch_shapes=[
@@ -261,7 +276,7 @@
     n_freq = lax.axis_size(FREQ)
     per_dev = bins.shape[0] // n_freq
     count = float(n_pts * n_freq * lax.axis_size(PTS) * n_var)
-    gram, high, low, tab = spectra(
+    gram, left, right, tab = spectra(
         starts, bins[None], weights[None], jnp.transpose(snapshots, (1, 0, 2)), 1
     )
     vmem = pltpu.VMEM
@@ -279,7 +294,7 @@
         out_specs=[in_vmem] * 2,
         out_shape=[vmem((KF * rows, LANES), jnp.float32), vmem((1, per_dev), jnp.float32)],
         name="modes",
-    )(keep(gram), keep(tab), keep(high), keep(low))
+    )(keep(gram), keep(tab), keep(left), keep(right))
     groups = per_dev * n_var
     modes = modes.reshape(n_freq, groups, 2 * tiles, LANES)
     modes = lax.all_to_all(modes, FREQ, 0, 0, tiled=True)

time: 56.9 us -> 57.2 us (level)
  no operation moved by 1% of the time
where the time goes in v5:
time: 57.2 us; the launch traced here: 57 us
  blocking collectives  41.7 us (73%)
  Pallas kernels  5.05 us (9%)
  waiting for transfers between devices  4.96 us (9%)
  starting transfers between devices  4.67 us (8%)
  between operations  0.66 us (1%)
    all_to_all x1, blocking collectives, body(): modes = lax.all_to_all(modes, FREQ, 0, 0, tiled=True)  21.4 us
    all_to_all x1, blocking collectives, body(): gram = lax.all_to_all(gram, FREQ, 0, 0, tiled=True)  20.3 us
    ppermute x3, waiting for transfers between devices, body(): lax.ppermute(gram, axis, [(i, i ^ flip) for i in range(lax.axis_size(axis...  4.96 us
    ppermute x3, starting transfers between devices, body(): lax.ppermute(gram, axis, [(i, i ^ flip) for i in range(lax.axis_size(axis...  4.67 us
    pallas_call x1, Pallas kernels, spectra(): pl.pallas_call(spectra_kernel, in_specs=[spec(memory_space=pl.ANY)] * 4,...  2.89 us
    pallas_call x1, Pallas kernels, body(): pl.pallas_call(functools.partial(modes_kernel, count), in_specs=[in_vmem]...  1.22 us
  transfers between devices with their start and end apart: 3, of which 3 were waited for; matrix products, arithmetic and copies ran while one was open for 0% of the time, Pallas kernels for 0%

profile of v5, /device:TPU:32, one launch (start us, length us, event | category | flops | bytes accessed | tf_op | source)
XLA Modules:
  0.0 57.0 jit_solution(7579683786097047576)
XLA Ops:
  0.6 2.9 %spectra.1 = (f32[1,1,576]{2,1,0:T(1,128)S(1)}, f32[5,256,128]{2,1,0:T(8,128)S(1)}, f32[5,256,128]{2,1,0:T(8,128)S(1)}, f32[6,64,256]{2,1,0:T(8,128)S(1)}) custom-call(s32[3]{0:T(128)} %starts_hbm.1, s32[1,64]{1,0:T(1,128)} %bitcast.13, f32[1,256]{1,0:T(1,128)} %bitcast.12, f32[5,256,256]{2,1,0:T(8,128)} %bitcast.11), custom_call_target="tpu_custom_call" | custom-call | tf_op jit(solution)/shard_map/spectra/pallas_call | solution.py:250
  3.5 0.1 collective-permute-start
  3.6 1.2 %collective-permute-done.two_ref = f32[1,1,576]{2,1,0:T(1,128)S(1)} collective-permute-done((f32[1,1,576]{2,1,0:T(1,128)S(1)}, f32[1,1,576]{2,1,0:T(1,128)S(1)}, u32[]{:S(2)}, u32[]{:S(2)}) %collective-permute-start) | collective-permute-done | bytes 2336 | tf_op jit(solution)/shard_map/ppermute | solution.py:287
  4.8 1.6 %collective-permute-start.1 = (f32[1,1,576]{2,1,0:T(1,128)S(1)}, f32[1,1,576]{2,1,0:T(1,128)S(1)}, u32[]{:S(2)}, u32[]{:S(2)}) collective-permute-start(f32[1,1,576]{2,1,0:T(1,128)S(1)} %add.3.one_ref), channel_id=1, source_target_pairs={{0,2},{2,0},{4,6},{6,4},{1,3},{3,1},{5,7},{7,5},{8,10},{10,8},{12,... | collective-permute-start | bytes 6920 | tf_op jit(solution)/shard_map/ppermute | solution.py:287
  6.4 2.0 %collective-permute-done.1.two_ref = f32[1,1,576]{2,1,0:T(1,128)S(1)} collective-permute-done((f32[1,1,576]{2,1,0:T(1,128)S(1)}, f32[1,1,576]{2,1,0:T(1,128)S(1)}, u32[]{:S(2)}, u32[]{:S(2)}) %collective-permute-start.1) | collective-permute-done | bytes 2336 | tf_op jit(solution)/shard_map/ppermute | solution.py:287
  8.4 3.0 %collective-permute-start.2 = (f32[1,1,576]{2,1,0:T(1,128)S(1)}, f32[1,1,576]{2,1,0:T(1,128)S(1)}, u32[]{:S(2)}, u32[]{:S(2)}) collective-permute-start(f32[1,1,576]{2,1,0:T(1,128)S(1)} %add.4.one_ref), channel_id=1, source_target_pairs={{0,6},{2,4},{4,2},{6,0},{1,7},{3,5},{5,3},{7,1},{8,14},{10,12},{12... | collective-permute-start | bytes 6920 | tf_op jit(solution)/shard_map/ppermute | solution.py:287
  11.4 1.8 %collective-permute-done.2.two_ref = f32[1,1,576]{2,1,0:T(1,128)S(1)} collective-permute-done((f32[1,1,576]{2,1,0:T(1,128)S(1)}, f32[1,1,576]{2,1,0:T(1,128)S(1)}, u32[]{:S(2)}, u32[]{:S(2)}) %collective-permute-start.2) | collective-permute-done | bytes 2336 | tf_op jit(solution)/shard_map/ppermute | solution.py:287
  13.2 20.3 %all_to_all.10.in_ref = f32[32,1,576]{2,1,0:T(1,128)S(1)} all-to-all(f32[32,1,576]{2,1,0:T(1,128)S(1)} %add.5), channel_id=1, replica_groups=mesh['freq_0'=4,'freq_1'=8,'pts_0'=4,'pts_1'=2] {'freq_0','freq_1'}, dimensions={0} | all-to-all | bytes 147456 | tf_op jit(solution)/shard_map/all_to_all | solution.py:289
  33.5 1.2 %modes.1 = (f32[1280,128]{1,0:T(8,128)S(1)}, f32[1,2]{1,0:T(1,128)S(1)}) custom-call(f32[32,1,576]{2,1,0:T(1,128)S(1)} %all_to_all.10.in_ref, f32[6,64,256]{2,1,0:T(8,128)S(1)} %get-tuple-element.11.tab_ref, f32[5,256,128]{2,1,0:T(8,128)S(1)} %get-tuple-element.12.left_ref, f32[5,256,128]{2,1,0:T(8,128)S(1)} %get-tuple-element.13.right_ref), custom_call_target="tpu_custom_call" | custom-call | tf_op jit(solution)/shard_map/modes/pallas_call | solution.py:291
  34.7 21.4 %all_to_all.11.in_ref = f32[32,10,4,128]{3,2,1,0:T(4,128)S(1)} all-to-all(f32[32,10,4,128]{3,2,1,0:T(4,128)S(1)} %bitcast.10), channel_id=1, replica_groups=mesh['freq_0'=4,'freq_1'=8,'pts_0'=4,'pts_1'=2] {'freq_0','freq_1'}, dimensions={0} | all-to-all | bytes 1310720 | tf_op jit(solution)/shard_map/all_to_all | solution.py:300
  56.1 0.9 %assemble.1 = (f32[10,32,4,128]{3,2,1,0:T(4,128)}, f32[1,2]{1,0:T(1,128)}) custom-call(f32[32,10,4,128]{3,2,1,0:T(4,128)S(1)} %all_to_all.11.in_ref, f32[1,2]{1,0:T(1,128)S(1)} %get-tuple-element.15.energy_ref), custom_call_target="tpu_custom_call" | custom-call | tf_op jit(solution)/shard_map/assemble/pallas_call | solution.py:301
  (3 shorter events, 0.0 us)
Async XLA Ops:
  3.5 1.3 %collective-permute-start = (f32[1,1,576]{2,1,0:T(1,128)S(1)}, f32[1,1,576]{2,1,0:T(1,128)S(1)}, u32[]{:S(2)}, u32[]{:S(2)}) collective-permute-start(f32[1,1,576]{2,1,0:T(1,128)S(1)} %get-tuple-element.10.one_ref), channel_id=1, source_target_pairs={{0,1},{1,0},{2,3},{3,2},{4,5},{5,4},{6,7},{7,6},{8,9},{9,8},{10,11... | collective-permute-start | bytes 6920 | tf_op jit(solution)/shard_map/ppermute | solution.py:287
  4.8 3.6 %collective-permute-start.1 = (f32[1,1,576]{2,1,0:T(1,128)S(1)}, f32[1,1,576]{2,1,0:T(1,128)S(1)}, u32[]{:S(2)}, u32[]{:S(2)}) collective-permute-start(f32[1,1,576]{2,1,0:T(1,128)S(1)} %add.3.one_ref), channel_id=1, source_target_pairs={{0,2},{2,0},{4,6},{6,4},{1,3},{3,1},{5,7},{7,5},{8,10},{10,8},{12,... | collective-permute-start | bytes 6920 | tf_op jit(solution)/shard_map/ppermute | solution.py:287
  8.4 4.8 %collective-permute-start.2 = (f32[1,1,576]{2,1,0:T(1,128)S(1)}, f32[1,1,576]{2,1,0:T(1,128)S(1)}, u32[]{:S(2)}, u32[]{:S(2)}) collective-permute-start(f32[1,1,576]{2,1,0:T(1,128)S(1)} %add.4.one_ref), channel_id=1, source_target_pairs={{0,6},{2,4},{4,2},{6,0},{1,7},{3,5},{5,3},{7,1},{8,14},{10,12},{12... | collective-permute-start | bytes 6920 | tf_op jit(solution)/shard_map/ppermute | solution.py:287

commit v6 on v5

--- a/solution.py
+++ b/solution.py
@@ -190,8 +190,11 @@
     )(keep(one), keep(two))
 
 
-def modes_kernel(count, in_ref, tab_ref, left_ref, right_ref, modes_ref, energy_ref):
+def modes_kernel(count, in_ref, tab_ref, left_ref, right_ref, modes_ref, energy_ref, split_ref):
     n_var, n_time, n_pts = left_ref.shape[0], left_ref.shape[1], 2 * left_ref.shape[2]
+    for v in range(n_var):
+        for i, part in enumerate(thirds(jnp.concatenate([left_ref[v], right_ref[v]], axis=1))):
+            split_ref[i, v] = part
     total = jnp.sum(in_ref[...], axis=0) * (1.0 / count)
     wide = []
     for first in range(0, QS * KF, LANES):
@@ -222,8 +225,7 @@
     tiles = n_pts // LANES
     stride = 2 * n_var * tiles
     for v in range(n_var):
-        centered = jnp.concatenate([left_ref[v], right_ref[v]], axis=1)
-        out = fine_product(m_parts, thirds(centered))
+        out = fine_product(m_parts, [split_ref[i, v] for i in range(3)])
         for t in range(tiles):
             for c in range(2):
                 modes_ref[pl.ds(2 * (v * tiles + t) + c, KF, stride), :] = out[
@@ -293,6 +295,7 @@
         in_specs=[in_vmem] * 4,
         out_specs=[in_vmem] * 2,
         out_shape=[vmem((KF * rows, LANES), jnp.float32), vmem((1, per_dev), jnp.float32)],
+        scratch_shapes=[vmem((3, n_var, n_time, n_pts), jnp.bfloat16)],
         name="modes",
     )(keep(gram), keep(tab), keep(left), keep(right))
     groups = per_dev * n_var

time: 57.2 us -> 57.2 us (level)
  no operation moved by 1% of the time
where the time goes in v6:
time: 57.2 us; the launch traced here: 57 us
  blocking collectives  41.7 us (73%)
  Pallas kernels  5.05 us (9%)
  waiting for transfers between devices  4.96 us (9%)
  starting transfers between devices  4.67 us (8%)
  between operations  0.66 us (1%)
    all_to_all x1, blocking collectives, body(): modes = lax.all_to_all(modes, FREQ, 0, 0, tiled=True)  21.4 us
    all_to_all x1, blocking collectives, body(): gram = lax.all_to_all(gram, FREQ, 0, 0, tiled=True)  20.3 us
    ppermute x3, waiting for transfers between devices, body(): lax.ppermute(gram, axis, [(i, i ^ flip) for i in range(lax.axis_size(axis...  4.96 us
    ppermute x3, starting transfers between devices, body(): lax.ppermute(gram, axis, [(i, i ^ flip) for i in range(lax.axis_size(axis...  4.67 us
    pallas_call x1, Pallas kernels, spectra(): pl.pallas_call(spectra_kernel, in_specs=[spec(memory_space=pl.ANY)] * 4,...  2.89 us
    pallas_call x1, Pallas kernels, body(): pl.pallas_call(functools.partial(modes_kernel, count), in_specs=[in_vmem]...  1.22 us
  transfers between devices with their start and end apart: 3, of which 3 were waited for; matrix products, arithmetic and copies ran while one was open for 0% of the time, Pallas kernels for 0%

profile of v6, /device:TPU:32, one launch (start us, length us, event | category | flops | bytes accessed | tf_op | source)
XLA Modules:
  0.0 57.0 jit_solution(7579683786097047576)
XLA Ops:
  0.6 2.9 %spectra.1 = (f32[1,1,576]{2,1,0:T(1,128)S(1)}, f32[5,256,128]{2,1,0:T(8,128)S(1)}, f32[5,256,128]{2,1,0:T(8,128)S(1)}, f32[6,64,256]{2,1,0:T(8,128)S(1)}) custom-call(s32[3]{0:T(128)} %starts_hbm.1, s32[1,64]{1,0:T(1,128)} %bitcast.13, f32[1,256]{1,0:T(1,128)} %bitcast.12, f32[5,256,256]{2,1,0:T(8,128)} %bitcast.11), custom_call_target="tpu_custom_call" | custom-call | tf_op jit(solution)/shard_map/spectra/pallas_call | solution.py:252
  3.5 0.1 collective-permute-start
  3.6 1.2 %collective-permute-done.two_ref = f32[1,1,576]{2,1,0:T(1,128)S(1)} collective-permute-done((f32[1,1,576]{2,1,0:T(1,128)S(1)}, f32[1,1,576]{2,1,0:T(1,128)S(1)}, u32[]{:S(2)}, u32[]{:S(2)}) %collective-permute-start) | collective-permute-done | bytes 2336 | tf_op jit(solution)/shard_map/ppermute | solution.py:289
  4.8 1.6 %collective-permute-start.1 = (f32[1,1,576]{2,1,0:T(1,128)S(1)}, f32[1,1,576]{2,1,0:T(1,128)S(1)}, u32[]{:S(2)}, u32[]{:S(2)}) collective-permute-start(f32[1,1,576]{2,1,0:T(1,128)S(1)} %add.3.one_ref), channel_id=1, source_target_pairs={{0,2},{2,0},{4,6},{6,4},{1,3},{3,1},{5,7},{7,5},{8,10},{10,8},{12,... | collective-permute-start | bytes 6920 | tf_op jit(solution)/shard_map/ppermute | solution.py:289
  6.4 2.0 %collective-permute-done.1.two_ref = f32[1,1,576]{2,1,0:T(1,128)S(1)} collective-permute-done((f32[1,1,576]{2,1,0:T(1,128)S(1)}, f32[1,1,576]{2,1,0:T(1,128)S(1)}, u32[]{:S(2)}, u32[]{:S(2)}) %collective-permute-start.1) | collective-permute-done | bytes 2336 | tf_op jit(solution)/shard_map/ppermute | solution.py:289
  8.4 3.0 %collective-permute-start.2 = (f32[1,1,576]{2,1,0:T(1,128)S(1)}, f32[1,1,576]{2,1,0:T(1,128)S(1)}, u32[]{:S(2)}, u32[]{:S(2)}) collective-permute-start(f32[1,1,576]{2,1,0:T(1,128)S(1)} %add.4.one_ref), channel_id=1, source_target_pairs={{0,6},{2,4},{4,2},{6,0},{1,7},{3,5},{5,3},{7,1},{8,14},{10,12},{12... | collective-permute-start | bytes 6920 | tf_op jit(solution)/shard_map/ppermute | solution.py:289
  11.4 1.8 %collective-permute-done.2.two_ref = f32[1,1,576]{2,1,0:T(1,128)S(1)} collective-permute-done((f32[1,1,576]{2,1,0:T(1,128)S(1)}, f32[1,1,576]{2,1,0:T(1,128)S(1)}, u32[]{:S(2)}, u32[]{:S(2)}) %collective-permute-start.2) | collective-permute-done | bytes 2336 | tf_op jit(solution)/shard_map/ppermute | solution.py:289
  13.2 20.3 %all_to_all.10.in_ref = f32[32,1,576]{2,1,0:T(1,128)S(1)} all-to-all(f32[32,1,576]{2,1,0:T(1,128)S(1)} %add.5), channel_id=1, replica_groups=mesh['freq_0'=4,'freq_1'=8,'pts_0'=4,'pts_1'=2] {'freq_0','freq_1'}, dimensions={0} | all-to-all | bytes 147456 | tf_op jit(solution)/shard_map/all_to_all | solution.py:291
  33.5 1.2 %modes.1 = (f32[1280,128]{1,0:T(8,128)S(1)}, f32[1,2]{1,0:T(1,128)S(1)}) custom-call(f32[32,1,576]{2,1,0:T(1,128)S(1)} %all_to_all.10.in_ref, f32[6,64,256]{2,1,0:T(8,128)S(1)} %get-tuple-element.11.tab_ref, f32[5,256,128]{2,1,0:T(8,128)S(1)} %get-tuple-element.12.left_ref, f32[5,256,128]{2,1,0:T(8,128)S(1)} %get-tuple-element.13.right_ref), custom_call_target="tpu_custom_call" | custom-call | tf_op jit(solution)/shard_map/modes/pallas_call | solution.py:293
  34.7 21.4 %all_to_all.11.in_ref = f32[32,10,4,128]{3,2,1,0:T(4,128)S(1)} all-to-all(f32[32,10,4,128]{3,2,1,0:T(4,128)S(1)} %bitcast.10), channel_id=1, replica_groups=mesh['freq_0'=4,'freq_1'=8,'pts_0'=4,'pts_1'=2] {'freq_0','freq_1'}, dimensions={0} | all-to-all | bytes 1310720 | tf_op jit(solution)/shard_map/all_to_all | solution.py:303
  56.1 0.9 %assemble.1 = (f32[10,32,4,128]{3,2,1,0:T(4,128)}, f32[1,2]{1,0:T(1,128)}) custom-call(f32[32,10,4,128]{3,2,1,0:T(4,128)S(1)} %all_to_all.11.in_ref, f32[1,2]{1,0:T(1,128)S(1)} %get-tuple-element.15.energy_ref), custom_call_target="tpu_custom_call" | custom-call | tf_op jit(solution)/shard_map/assemble/pallas_call | solution.py:304
  (3 shorter events, 0.0 us)
Async XLA Ops:
  3.5 1.3 %collective-permute-start = (f32[1,1,576]{2,1,0:T(1,128)S(1)}, f32[1,1,576]{2,1,0:T(1,128)S(1)}, u32[]{:S(2)}, u32[]{:S(2)}) collective-permute-start(f32[1,1,576]{2,1,0:T(1,128)S(1)} %get-tuple-element.10.one_ref), channel_id=1, source_target_pairs={{0,1},{1,0},{2,3},{3,2},{4,5},{5,4},{6,7},{7,6},{8,9},{9,8},{10,11... | collective-permute-start | bytes 6920 | tf_op jit(solution)/shard_map/ppermute | solution.py:289
  4.8 3.6 %collective-permute-start.1 = (f32[1,1,576]{2,1,0:T(1,128)S(1)}, f32[1,1,576]{2,1,0:T(1,128)S(1)}, u32[]{:S(2)}, u32[]{:S(2)}) collective-permute-start(f32[1,1,576]{2,1,0:T(1,128)S(1)} %add.3.one_ref), channel_id=1, source_target_pairs={{0,2},{2,0},{4,6},{6,4},{1,3},{3,1},{5,7},{7,5},{8,10},{10,8},{12,... | collective-permute-start | bytes 6920 | tf_op jit(solution)/shard_map/ppermute | solution.py:289
  8.4 4.8 %collective-permute-start.2 = (f32[1,1,576]{2,1,0:T(1,128)S(1)}, f32[1,1,576]{2,1,0:T(1,128)S(1)}, u32[]{:S(2)}, u32[]{:S(2)}) collective-permute-start(f32[1,1,576]{2,1,0:T(1,128)S(1)} %add.4.one_ref), channel_id=1, source_target_pairs={{0,6},{2,4},{4,2},{6,0},{1,7},{3,5},{5,3},{7,1},{8,14},{10,12},{12... | collective-permute-start | bytes 6920 | tf_op jit(solution)/shard_map/ppermute | solution.py:289

commit v7 on v6

--- a/solution.py
+++ b/solution.py
@@ -117,20 +117,26 @@
         left_ref[v], right_ref[v] = centered[:, : n_pts // 2], centered[:, n_pts // 2 :]
         high, low = halves(centered)
         spec_ref[v] = product(t_high, t_low, high, low)
+        if v % 2 == 0 and v < n_var - 1:
+            continue
+        group = [v] if v % 2 == 0 else [v - 1, v]
         for first in range(0, KF, 8):
             for lane in range(0, n_pts, LANES):
-                s = [
-                    spec_ref[v, KF * r + first : KF * r + first + 8, lane : lane + LANES]
-                    for r in range(2 * NB)
-                ]
-                re, im = s[0::2], s[1::2]
-                parts = [re[a] * re[a] + im[a] * im[a] for a in range(NB)]
-                parts += [re[a] * re[c] + im[a] * im[c] for a, c in PAIRS]
-                parts += [re[a] * im[c] - im[a] * re[c] for a, c in PAIRS]
+                total = None
+                for u in group:
+                    s = [
+                        spec_ref[u, KF * r + first : KF * r + first + 8, lane : lane + LANES]
+                        for r in range(2 * NB)
+                    ]
+                    re, im = s[0::2], s[1::2]
+                    parts = [re[a] * re[a] + im[a] * im[a] for a in range(NB)]
+                    parts += [re[a] * re[c] + im[a] * im[c] for a, c in PAIRS]
+                    parts += [re[a] * im[c] - im[a] * re[c] for a, c in PAIRS]
+                    total = parts if total is None else [p + t for p, t in zip(parts, total)]
                 for q in range(QS):
-                    if v > 0:
-                        parts[q] = parts[q] + sum_ref[q, first : first + 8, lane : lane + LANES]
-                    sum_ref[q, first : first + 8, lane : lane + LANES] = parts[q]
+                    if group[0] > 0:
+                        total[q] = total[q] + sum_ref[q, first : first + 8, lane : lane + LANES]
+                    sum_ref[q, first : first + 8, lane : lane + LANES] = total[q]
     weighted = sum_ref[...] * wts_ref[...][None]
     prod = sum(weighted[:, :, lane : lane + LANES] for lane in range(0, n_pts, LANES))
     prod = prod.reshape(QS * KF, LANES)

time: 57.2 us -> 57.2 us (level)
  no operation moved by 1% of the time
where the time goes in v7:
time: 57.2 us; the launch traced here: 57 us
  blocking collectives  41.7 us (73%)
  Pallas kernels  5.04 us (9%)
  waiting for transfers between devices  4.96 us (9%)
  starting transfers between devices  4.67 us (8%)
  between operations  0.66 us (1%)
    all_to_all x1, blocking collectives, body(): modes = lax.all_to_all(modes, FREQ, 0, 0, tiled=True)  21.4 us
    all_to_all x1, blocking collectives, body(): gram = lax.all_to_all(gram, FREQ, 0, 0, tiled=True)  20.3 us
    ppermute x3, waiting for transfers between devices, body(): lax.ppermute(gram, axis, [(i, i ^ flip) for i in range(lax.axis_size(axis...  4.96 us
    ppermute x3, starting transfers between devices, body(): lax.ppermute(gram, axis, [(i, i ^ flip) for i in range(lax.axis_size(axis...  4.67 us
    pallas_call x1, Pallas kernels, spectra(): pl.pallas_call(spectra_kernel, in_specs=[spec(memory_space=pl.ANY)] * 4,...  2.89 us
    pallas_call x1, Pallas kernels, body(): pl.pallas_call(functools.partial(modes_kernel, count), in_specs=[in_vmem]...  1.21 us
  transfers between devices with their start and end apart: 3, of which 3 were waited for; matrix products, arithmetic and copies ran while one was open for 0% of the time, Pallas kernels for 0%

profile of v7, /device:TPU:32, one launch (start us, length us, event | category | flops | bytes accessed | tf_op | source)
XLA Modules:
  0.0 57.0 jit_solution(5232840348881159497)
XLA Ops:
  0.6 2.9 %spectra.1 = (f32[1,1,576]{2,1,0:T(1,128)S(1)}, f32[5,256,128]{2,1,0:T(8,128)S(1)}, f32[5,256,128]{2,1,0:T(8,128)S(1)}, f32[6,64,256]{2,1,0:T(8,128)S(1)}) custom-call(s32[3]{0:T(128)} %starts_hbm.1, s32[1,64]{1,0:T(1,128)} %bitcast.13, f32[1,256]{1,0:T(1,128)} %bitcast.12, f32[5,256,256]{2,1,0:T(8,128)} %bitcast.11), custom_call_target="tpu_custom_call" | custom-call | tf_op jit(solution)/shard_map/spectra/pallas_call | solution.py:258
  3.5 0.1 collective-permute-start
  3.6 1.2 %collective-permute-done.two_ref = f32[1,1,576]{2,1,0:T(1,128)S(1)} collective-permute-done((f32[1,1,576]{2,1,0:T(1,128)S(1)}, f32[1,1,576]{2,1,0:T(1,128)S(1)}, u32[]{:S(2)}, u32[]{:S(2)}) %collective-permute-start) | collective-permute-done | bytes 2336 | tf_op jit(solution)/shard_map/ppermute | solution.py:295
  4.8 1.6 %collective-permute-start.1 = (f32[1,1,576]{2,1,0:T(1,128)S(1)}, f32[1,1,576]{2,1,0:T(1,128)S(1)}, u32[]{:S(2)}, u32[]{:S(2)}) collective-permute-start(f32[1,1,576]{2,1,0:T(1,128)S(1)} %add.3.one_ref), channel_id=1, source_target_pairs={{0,2},{2,0},{4,6},{6,4},{1,3},{3,1},{5,7},{7,5},{8,10},{10,8},{12,... | collective-permute-start | bytes 6920 | tf_op jit(solution)/shard_map/ppermute | solution.py:295
  6.4 2.0 %collective-permute-done.1.two_ref = f32[1,1,576]{2,1,0:T(1,128)S(1)} collective-permute-done((f32[1,1,576]{2,1,0:T(1,128)S(1)}, f32[1,1,576]{2,1,0:T(1,128)S(1)}, u32[]{:S(2)}, u32[]{:S(2)}) %collective-permute-start.1) | collective-permute-done | bytes 2336 | tf_op jit(solution)/shard_map/ppermute | solution.py:295
  8.4 3.0 %collective-permute-start.2 = (f32[1,1,576]{2,1,0:T(1,128)S(1)}, f32[1,1,576]{2,1,0:T(1,128)S(1)}, u32[]{:S(2)}, u32[]{:S(2)}) collective-permute-start(f32[1,1,576]{2,1,0:T(1,128)S(1)} %add.4.one_ref), channel_id=1, source_target_pairs={{0,6},{2,4},{4,2},{6,0},{1,7},{3,5},{5,3},{7,1},{8,14},{10,12},{12... | collective-permute-start | bytes 6920 | tf_op jit(solution)/shard_map/ppermute | solution.py:295
  11.4 1.8 %collective-permute-done.2.two_ref = f32[1,1,576]{2,1,0:T(1,128)S(1)} collective-permute-done((f32[1,1,576]{2,1,0:T(1,128)S(1)}, f32[1,1,576]{2,1,0:T(1,128)S(1)}, u32[]{:S(2)}, u32[]{:S(2)}) %collective-permute-start.2) | collective-permute-done | bytes 2336 | tf_op jit(solution)/shard_map/ppermute | solution.py:295
  13.2 20.3 %all_to_all.10.in_ref = f32[32,1,576]{2,1,0:T(1,128)S(1)} all-to-all(f32[32,1,576]{2,1,0:T(1,128)S(1)} %add.5), channel_id=1, replica_groups=mesh['freq_0'=4,'freq_1'=8,'pts_0'=4,'pts_1'=2] {'freq_0','freq_1'}, dimensions={0} | all-to-all | bytes 147456 | tf_op jit(solution)/shard_map/all_to_all | solution.py:297
  33.5 1.2 %modes.1 = (f32[1280,128]{1,0:T(8,128)S(1)}, f32[1,2]{1,0:T(1,128)S(1)}) custom-call(f32[32,1,576]{2,1,0:T(1,128)S(1)} %all_to_all.10.in_ref, f32[6,64,256]{2,1,0:T(8,128)S(1)} %get-tuple-element.11.tab_ref, f32[5,256,128]{2,1,0:T(8,128)S(1)} %get-tuple-element.12.left_ref, f32[5,256,128]{2,1,0:T(8,128)S(1)} %get-tuple-element.13.right_ref), custom_call_target="tpu_custom_call" | custom-call | tf_op jit(solution)/shard_map/modes/pallas_call | solution.py:299
  34.7 21.4 %all_to_all.11.in_ref = f32[32,10,4,128]{3,2,1,0:T(4,128)S(1)} all-to-all(f32[32,10,4,128]{3,2,1,0:T(4,128)S(1)} %bitcast.10), channel_id=1, replica_groups=mesh['freq_0'=4,'freq_1'=8,'pts_0'=4,'pts_1'=2] {'freq_0','freq_1'}, dimensions={0} | all-to-all | bytes 1310720 | tf_op jit(solution)/shard_map/all_to_all | solution.py:309
  56.1 0.9 %assemble.1 = (f32[10,32,4,128]{3,2,1,0:T(4,128)}, f32[1,2]{1,0:T(1,128)}) custom-call(f32[32,10,4,128]{3,2,1,0:T(4,128)S(1)} %all_to_all.11.in_ref, f32[1,2]{1,0:T(1,128)S(1)} %get-tuple-element.15.energy_ref), custom_call_target="tpu_custom_call" | custom-call | tf_op jit(solution)/shard_map/assemble/pallas_call | solution.py:310
  (3 shorter events, 0.0 us)
Async XLA Ops:
  3.5 1.3 %collective-permute-start = (f32[1,1,576]{2,1,0:T(1,128)S(1)}, f32[1,1,576]{2,1,0:T(1,128)S(1)}, u32[]{:S(2)}, u32[]{:S(2)}) collective-permute-start(f32[1,1,576]{2,1,0:T(1,128)S(1)} %get-tuple-element.10.one_ref), channel_id=1, source_target_pairs={{0,1},{1,0},{2,3},{3,2},{4,5},{5,4},{6,7},{7,6},{8,9},{9,8},{10,11... | collective-permute-start | bytes 6920 | tf_op jit(solution)/shard_map/ppermute | solution.py:295
  4.8 3.6 %collective-permute-start.1 = (f32[1,1,576]{2,1,0:T(1,128)S(1)}, f32[1,1,576]{2,1,0:T(1,128)S(1)}, u32[]{:S(2)}, u32[]{:S(2)}) collective-permute-start(f32[1,1,576]{2,1,0:T(1,128)S(1)} %add.3.one_ref), channel_id=1, source_target_pairs={{0,2},{2,0},{4,6},{6,4},{1,3},{3,1},{5,7},{7,5},{8,10},{10,8},{12,... | collective-permute-start | bytes 6920 | tf_op jit(solution)/shard_map/ppermute | solution.py:295
  8.4 4.8 %collective-permute-start.2 = (f32[1,1,576]{2,1,0:T(1,128)S(1)}, f32[1,1,576]{2,1,0:T(1,128)S(1)}, u32[]{:S(2)}, u32[]{:S(2)}) collective-permute-start(f32[1,1,576]{2,1,0:T(1,128)S(1)} %add.4.one_ref), channel_id=1, source_target_pairs={{0,6},{2,4},{4,2},{6,0},{1,7},{3,5},{5,3},{7,1},{8,14},{10,12},{12... | collective-permute-start | bytes 6920 | tf_op jit(solution)/shard_map/ppermute | solution.py:295
